TPU v7x, 256 devices: a whole 4x4x8 slice. The times are simulated.
256 devices in a mesh: macro: 128 (over y, x_lo, z, core), micro: 2 (over x_hi).
Axes of the slice: x: 4 (x_hi: 2, x_lo: 2; x = x_hi * 2 + x_lo), y: 4, z: 8, core: 2. Of those that a mesh axis runs over, the one named last changes fastest.
Arguments:
- macro_state: float32 [65536, 128], P('macro'), may hold values from -6 to 6
- micro_state: bfloat16 [65536, 12, 512], P('macro', None, 'micro'), may hold values from -6 to 6
- velocity: float32 [65536], P('macro'), may hold values from 0.25 to 4
- propagator: bfloat16 [512, 512], P(None, 'micro'), may hold values from -1 to 1
- forcing_map: float32 [128, 512], P(None, 'micro'), may hold values from -0.5 to 0.5
- readout: float32 [128, 512], P(None, 'micro'), may hold values from -1 to 1
- speed_weights: float32 [128], replicated, may hold values from -0.5 to 0.5
Outputs:
- macro_next: float32 [65536, 128], P('macro')
- micro_final: bfloat16 [65536, 12, 512], P('macro', None, 'micro')
All inputs are finite; a program needn't handle non-finite values.
Results may differ from a plain program's by a relative error of at most 0.006.
Values may be sent and summed in bfloat16 or wider, within the bound.
No kernel may reach another device: no remote copies, remote signals or barrier semaphores. Data moves between devices by JAX's collectives and lax.ppermute only.
A program may use at most 64 MiB of HBM per device.

v0:
```python
import jax
import jax.numpy as jnp
from jax import lax
from jax.sharding import Mesh
from jax.sharding import PartitionSpec as P

S = 12
STEPS = 4
MACRO = ("macro_0", "macro_1", "macro_2", "macro_3")


def laid_out(blocks, dim):
    blocks = jnp.moveaxis(blocks, 0, dim)
    dims = blocks.shape
    return blocks.reshape(*dims[:dim], dims[dim] * dims[dim + 1], *dims[dim + 2 :])


def sent_to_all(array, axis):
    copies = jnp.broadcast_to(array, (lax.axis_size(axis), *array.shape))
    return lax.all_to_all(copies, axis, split_axis=0, concat_axis=0, tiled=True)


def gathered_copies(array, axis, dim):
    return laid_out(sent_to_all(array, axis), dim)


def side_by_side(arrays, axis, dim, along):
    widths = [a.shape[along] for a in arrays]
    both = jnp.concatenate(arrays, axis=along)
    result = gathered_copies(both, axis, dim)
    return tuple(jnp.split(result, [sum(widths[:k]) for k in range(1, len(widths))], axis=along))


def taken_together(array, axis):
    everything = sent_to_all(array, axis)
    return jnp.sum(everything.astype(jnp.float32), axis=0)


def cut_along(array, dim, size):
    before, after = (array.shape[:dim], array.shape[dim + 1 :])
    return jnp.moveaxis(array.reshape(*before, size, -1, *after), dim, 0)


def piece_ends(length, count):
    unit = 8 if length >= 8 * count else 1
    return [length // unit * k // count * unit for k in range(1, count)]


def cut_exchange(array, axis, pieces, split_dim, concat_dim):
    blocks = cut_along(array, split_dim, lax.axis_size(axis))
    split_at = max(range(1, max(2, blocks.ndim - 1)), key=lambda d: blocks.shape[d])
    outs = []
    for section in jnp.split(blocks, piece_ends(blocks.shape[split_at], pieces), axis=split_at):
        if section.size:
            outs.append(lax.all_to_all(section, axis, split_axis=0, concat_axis=0, tiled=True))
    return laid_out(jnp.concatenate(outs, axis=split_at), concat_dim)


def by_axis(array, axes):
    for axis in axes:
        array = lax.pmax(array, axis)
    return array


def from_behind(value, axis, steps):
    count = lax.axis_size(axis)
    pairs = [(source, (source + steps) % count) for source in range(count)]
    return lax.ppermute(value, axis, pairs)


def shards(macro_state, micro_state, velocity, propagator, forcing_map, readout, speed_weights):
    highest = lax.Precision.HIGHEST
    coupling = gathered_copies(propagator, "micro", 1)
    forcing_full, readout_full = side_by_side((forcing_map, readout), "micro", 1, 0)
    forcing = jnp.tanh(
        jnp.dot(macro_state, forcing_full, precision=highest, preferred_element_type=jnp.float32)
    )
    micro_now = lax.all_to_all(micro_state, "micro", split_axis=1, concat_axis=2, tiled=True)
    tanh_sum = jnp.zeros(forcing.shape, jnp.float32)
    width = micro_now.shape[2]
    for _ in range(STEPS):
        summed = jnp.dot(micro_now.reshape(-1, width), coupling, preferred_element_type=jnp.float32)
        summed = summed.reshape(micro_now.shape)
        micro_now = (summed + forcing[:, None, :]).astype(jnp.bfloat16)
        tanh_sum = tanh_sum + jnp.sum(jnp.tanh(micro_now.astype(jnp.float32)), axis=1)
    partial_value = jnp.dot(
        tanh_sum / (STEPS * S),
        readout_full.T,
        precision=highest,
        preferred_element_type=jnp.float32,
    )
    forces = taken_together(partial_value.astype(jnp.bfloat16), "micro").astype(jnp.float32)
    micro_final = cut_exchange(micro_now, "micro", 2, 2, 1)
    drive_in = jnp.dot(forces, speed_weights, precision=highest, preferred_element_type=jnp.float32)
    speeds = velocity * (1.5 + jnp.tanh(drive_in))
    fastest = by_axis(jnp.max(speeds), MACRO)
    time_step = 0.8 / jnp.maximum(fastest, 1.0)
    fluxes = speeds[:, None] * macro_state
    stacked = jnp.stack([macro_state, fluxes])
    ahead_rows = from_behind(stacked[:, :1], MACRO, -1)
    state_after = jnp.concatenate([macro_state[1:], ahead_rows[0]], axis=0)
    flux_after = jnp.concatenate([fluxes[1:], ahead_rows[1]], axis=0)
    interface = 0.5 * (fluxes + flux_after) - 0.5 * fastest * (state_after - macro_state)
    carried = from_behind(interface[-1:], MACRO, 1)
    interface_before = jnp.concatenate([carried, interface[:-1]], axis=0)
    macro_next = macro_state - time_step * (interface - interface_before) + time_step * forces
    return (macro_next, micro_final)


def solution(mesh):
    torus = Mesh(
        mesh.devices.reshape(4, 2, 8, 2, mesh.shape["micro"]),
        ("macro_0", "macro_1", "macro_2", "macro_3", "micro"),
    )
    placed = (
        P(MACRO, None),
        P(MACRO, None, "micro"),
        P(MACRO),
        P(None, "micro"),
        P(None, "micro"),
        P(None, "micro"),
        P(),
    )
    return jax.shard_map(
        shards,
        mesh=torus,
        in_specs=placed,
        out_specs=(P(MACRO, None), P(MACRO, None, "micro")),
        check_vma=False,
    )
```

profile of v0, /device:TPU:4, one launch (start us, length us, event | category | flops | bytes accessed | tf_op | source)
XLA Modules:
  0.0 182.2 jit_solution(6250397391435274117)
XLA Ops:
  1.8 10.9 %all_to_all.40 = f32[2,256,256]{1,2,0:T(8,128)} all-to-all(f32[2,256,256]{1,2,0:T(8,128)S(1)} %broadcast_in_dim.7), channel_id=1, replica_groups=mesh['macro_0'=4,'macro_1'=2,'macro_2'=8,'macro_3'=2,'micro'=2] {'micro'}, dimensions={0} | all-to-all | bytes 1048576 | tf_op jit(solution)/shard_map/all_to_all | solution.py:20
  13.7 11.1 %all_to_all.41 = bf16[2,512,256]{2,1,0:T(8,128)(2,1)} all-to-all(bf16[2,512,256]{2,1,0:T(8,128)(2,1)S(1)} %broadcast_in_dim.6), channel_id=1, replica_groups=mesh['macro_0'=4,'macro_1'=2,'macro_2'=8,'macro_3'=2,'micro'=2] {'micro'}, dimensions={0} | all-to-all | bytes 1048576 | tf_op jit(solution)/shard_map/all_to_all | solution.py:20
  24.9 7.3 %all-to-all-start = ((bf16[512,12,256]{2,0,1:T(8,128)(2,1)}), bf16[512,12,256]{2,0,1:T(8,128)(2,1)S(1)}, u32[]{:S(2)}, u32[]{:S(2)}) async-start(bf16[512,12,256]{2,0,1:T(8,128)(2,1)} %param.8), calls=%async_computation | async-start | bytes 6291456 | tf_op jit(solution)/shard_map/all_to_all | solution.py:78
  32.1 2.4 %copy.28 = bf16[512,2,256]{2,1,0:T(2,128)(2,1)} copy(bf16[512,2,256]{2,0,1:T(8,128)(2,1)} %bitcast.53) | data formatting | bytes 1048576 | tf_op jit(solution)/shard_map/transpose | solution.py:13
  34.6 2.1 %copy.36 = bf16[512,2,256]{0,2,1:T(8,128)(2,1)} copy(bf16[512,2,256]{2,0,1:T(8,128)(2,1)} %bitcast.54) | data formatting | bytes 1048576 | tf_op jit(solution)/shard_map/reshape | solution.py:15
  36.6 1.8 fusion.18
  38.4 2.0 %fusion = f32[512,512]{0,1:T(8,128)} fusion(f32[128,512]{0,1:T(8,128)S(1)} %bitcast.60, f32[512,128]{1,0:T(8,128)S(1)} %copy-done.1), kind=kOutput, calls=%fused_computation.12 | convolution fusion | flops 402653184 | bytes 1572864 | tf_op jit(solution)/shard_map/dot_general | solution.py:76
  40.4 2.5 %copy.30 = f32[512,512]{1,0:T(8,128)} copy(f32[512,512]{0,1:T(8,128)} %fusion) | data formatting | bytes 2097152 | tf_op jit(solution)/shard_map/tanh | solution.py:75
  42.9 2.2 %reshape.38 = bf16[512,512,1]{1,0,2:T(8,128)(2,1)} reshape(bf16[512,2,256]{2,1,0:T(2,128)(2,1)} %copy.28) | data formatting | bytes 1048576 | tf_op jit(solution)/shard_map/reshape | solution.py:15
  45.1 18.7 %all-to-all-done = bf16[512,12,256]{2,0,1:T(8,128)(2,1)S(1)} async-done(((bf16[512,12,256]{2,0,1:T(8,128)(2,1)}), bf16[512,12,256]{2,0,1:T(8,128)(2,1)S(1)}, u32[]{:S(2)}, u32[]{:S(2)}) %all-to-all-start) | async-done | bytes 3145760 | tf_op jit(solution)/shard_map/all_to_all | solution.py:78
  63.8 4.9 %copy.42 = bf16[512,2,6,256]{3,1,0,2:T(2,128)(2,1)} copy(bf16[512,2,6,256]{3,0,2,1:T(8,128)(2,1)S(1)} %bitcast.49) | data formatting | bytes 6291456 | tf_op jit(solution)/shard_map/all_to_all | solution.py:78
  68.7 4.6 %dot_general.23 = bf16[512,6,512]{2,0,1:T(8,128)(2,1)S(1)} reshape(bf16[512,6,2,256]{3,2,0,1:T(2,128)(2,1)} %bitcast.51) | data formatting | bytes 6291456 | tf_op jit(solution)/shard_map/dot_general | solution.py:82
  73.3 3.8 %tanh_reduce_fusion.3 = (f32[512,512]{1,0:T(8,128)S(1)}, bf16[512,6,512]{2,0,1:T(8,128)(2,1)S(1)}) fusion(f32[512,512]{1,0:T(8,128)} %copy.30, bf16[512,6,512]{2,0,1:T(8,128)(2,1)S(1)} %dot_general.23, bf16[512,512,1]{1,0,2:T(8,128)(2,1)} %reshape.38), kind=kOutput, calls=%fused_computation.6 | convolution fusion | flops 1616642048 | bytes 8912896 | tf_op jit(solution)/shard_map/dot_general | solution.py:82
  77.1 2.1 %tanh_reduce_fusion.2 = (f32[512,512]{1,0:T(8,128)S(1)}, bf16[512,6,512]{2,0,1:T(8,128)(2,1)S(1)}) fusion(f32[512,512]{1,0:T(8,128)S(1)} %copy-done.4, bf16[512,6,512]{2,0,1:T(8,128)(2,1)S(1)} %get-tuple-element.17, bf16[512,512,1]{1,0,2:T(8,128)(2,1)S(1)} %copy-done.7), kind=kOutput, calls=%fused_computation.4 | convolution fusion | flops 1616642048 | bytes 8912896 | tf_op jit(solution)/shard_map/dot_general | solution.py:82
  79.2 2.1 %tanh_reduce_fusion.1 = (f32[512,512]{1,0:T(8,128)S(1)}, bf16[512,6,512]{2,0,1:T(8,128)(2,1)S(1)}) fusion(f32[512,512]{1,0:T(8,128)S(1)} %copy-done.4, bf16[512,6,512]{2,0,1:T(8,128)(2,1)S(1)} %get-tuple-element.19, bf16[512,512,1]{1,0,2:T(8,128)(2,1)S(1)} %copy-done.7), kind=kOutput, calls=%fused_computation.2 | convolution fusion | flops 1616642048 | bytes 8912896 | tf_op jit(solution)/shard_map/dot_general | solution.py:82
  81.3 2.1 %tanh_reduce_fusion = (f32[512,512]{1,0:T(8,128)S(1)}, bf16[512,6,512]{2,0,1:T(8,128)(2,1)S(1)}) fusion(f32[512,512]{1,0:T(8,128)S(1)} %copy-done.4, bf16[512,6,512]{2,0,1:T(8,128)(2,1)S(1)} %get-tuple-element.15, bf16[512,512,1]{0,1,2:T(8,128)(2,1)S(1)} %bitcast.61), kind=kOutput, calls=%fused_computation | convolution fusion | flops 1616642048 | bytes 8912896 | tf_op jit(solution)/shard_map/dot_general | solution.py:82
  83.4 1.0 convolution_convert_fusion
  85.2 7.3 %all-to-all-start.3 = ((bf16[2,512,128]{2,1,0:T(8,128)(2,1)}), bf16[2,512,128]{2,1,0:T(8,128)(2,1)}, u32[]{:S(2)}, u32[]{:S(2)}) async-start(bf16[2,512,128]{2,1,0:T(8,128)(2,1)} %broadcast_in_dim.16), calls=%async_computation.3 | async-start | bytes 524288 | tf_op jit(solution)/shard_map/all_to_all | solution.py:20
  92.8 2.0 %fusion.17 = (bf16[2,256,6,256]{3,1,2,0:T(8,128)(2,1)}, bf16[2,256,6,256]{3,1,2,0:T(8,128)(2,1)}) fusion(bf16[2,512,6,256]{3,1,2,0:T(8,128)(2,1)S(1)} %bitcast.50), kind=kLoop, calls=%fused_computation.40 | loop fusion | bytes 6291456 | tf_op jit(solution)/shard_map/split | solution.py:53
  95.8 7.2 %all-to-all-start.5 = ((bf16[2,256,6,256]{3,1,2,0:T(8,128)(2,1)}), bf16[2,256,6,256]{3,1,2,0:T(8,128)(2,1)S(1)}, u32[]{:S(2)}, u32[]{:S(2)}) async-start(bf16[2,256,6,256]{3,1,2,0:T(8,128)(2,1)} %get-tuple-element.5), calls=%async_computation.5 | async-start | bytes 3145728 | tf_op jit(solution)/shard_map/all_to_all | solution.py:55
  106.6 9.2 %all-to-all-done.5 = bf16[2,256,6,256]{3,1,2,0:T(8,128)(2,1)S(1)} async-done(((bf16[2,256,6,256]{3,1,2,0:T(8,128)(2,1)}), bf16[2,256,6,256]{3,1,2,0:T(8,128)(2,1)S(1)}, u32[]{:S(2)}, u32[]{:S(2)}) %all-to-all-start.5) | async-done | bytes 1572896 | tf_op jit(solution)/shard_map/all_to_all | solution.py:55
  115.8 6.9 %all-to-all-start.4 = ((bf16[2,256,6,256]{3,1,2,0:T(8,128)(2,1)}), bf16[2,256,6,256]{3,1,2,0:T(8,128)(2,1)S(1)}, u32[]{:S(2)}, u32[]{:S(2)}) async-start(bf16[2,256,6,256]{3,1,2,0:T(8,128)(2,1)} %get-tuple-element.4), calls=%async_computation.4 | async-start | bytes 3145728 | tf_op jit(solution)/shard_map/all_to_all | solution.py:55
  123.4 6.2 %collective-permute-start = (f32[2,1,128]{2,1,0:T(1,128)S(1)}, f32[2,1,128]{2,1,0:T(1,128)S(1)}, u32[]{:S(2)}, u32[]{:S(2)}) collective-permute-start(f32[2,1,128]{2,1,0:T(1,128)S(1)} %pad_maximum_fusion.2), channel_id=1, source_target_pairs={{0,254},{2,0},{4,2},{6,4},{8,6},{10,8},{12,10},{14,12},{16,14},{18... | collective-permute-start | bytes 3080 | tf_op jit(solution)/shard_map/ppermute | solution.py:68
  129.6 9.1 %pmax.28 = f32[]{:T(128)} all-reduce(f32[]{:T(128)} %get-tuple-element.2), channel_id=1, replica_groups=mesh['macro_0'=4,'macro_1'=2,'macro_2'=8,'macro_3'=2,'micro'=2] {'macro_0'}, use_global_device_ids=true, to_apply=%region_6.0 | all-reduce | flops 1 | bytes 8 | tf_op jit(solution)/shard_map/pmax | solution.py:61
  138.6 5.5 %pmax.29 = f32[]{:T(128)} all-reduce(f32[]{:T(128)} %pmax.28), channel_id=1, replica_groups=mesh['macro_0'=4,'macro_1'=2,'macro_2'=8,'macro_3'=2,'micro'=2] {'macro_1'}, use_global_device_ids=true, to_apply=%region_7.0 | all-reduce | flops 1 | bytes 8 | tf_op jit(solution)/shard_map/pmax | solution.py:61
  144.2 19.0 %pmax.30 = f32[]{:T(128)} all-reduce(f32[]{:T(128)} %pmax.29), channel_id=1, replica_groups=mesh['macro_0'=4,'macro_1'=2,'macro_2'=8,'macro_3'=2,'micro'=2] {'macro_2'}, use_global_device_ids=true, to_apply=%region_8.0 | all-reduce | flops 1 | bytes 8 | tf_op jit(solution)/shard_map/pmax | solution.py:61
  163.9 3.1 %pmax.31 = f32[]{:T(128)} all-reduce(f32[]{:T(128)} %pmax.30), channel_id=1, replica_groups=mesh['macro_0'=4,'macro_1'=2,'macro_2'=8,'macro_3'=2,'micro'=2] {'macro_3'}, use_global_device_ids=true, to_apply=%region_9.0 | all-reduce | flops 1 | bytes 8 | tf_op jit(solution)/shard_map/pmax | solution.py:61
  167.0 1.7 slice.30
  169.3 1.2 fusion.7
  172.0 6.4 %collective-permute-done.1 = f32[1,128]{1,0:T(1,128)S(1)} collective-permute-done((f32[1,128]{1,0:T(1,128)S(1)}, f32[1,128]{1,0:T(1,128)S(1)}, u32[]{:S(2)}, u32[]{:S(2)}) %collective-permute-start.1) | collective-permute-done | bytes 544 | tf_op jit(solution)/shard_map/ppermute | solution.py:68
  178.4 1.9 %fusion.11 = f32[512,128]{1,0:T(8,128)} fusion(f32[512,128]{1,0:T(8,128)S(1)} %copy-done.1, f32[512,128]{1,0:T(8,128)} %copy-done.3, f32[511,128]{1,0:T(8,128)} %bitcast.57, f32[1,128]{1,0:T(1,128)S(1)} %collective-permute-done.1, f32[512,128]{1,0:T(8,128)} %copy-done.2, f32[]{:T(128)S(6)} %div.11), kind=kLoop, calls=%fused_computation.29 | loop fusion | flops 393216 | bytes 1310724 | tf_op jit(solution)/shard_map/add | solution.py:106
  180.3 1.9 %pad_maximum_fusion = bf16[2,512,6,256]{3,1,2,0:T(8,128)(2,1)} fusion(bf16[2,256,6,256]{3,1,2,0:T(8,128)(2,1)S(1)} %all-to-all-done.5, bf16[2,256,6,256]{3,1,2,0:T(8,128)(2,1)S(1)} %all-to-all-done.4), kind=kLoop, calls=%fused_computation.9 | loop fusion | flops 6291456 | bytes 6291456 | tf_op jit(solution)/shard_map/concatenate | solution.py:56
  (36 shorter events, 10.0 us)
Async XLA Ops:
  0.6 104.1 %copy-start = (f32[128]{0:T(128)S(1)}, f32[128]{0:T(128)}, u32[]{:S(2)}) copy-start(f32[128]{0:T(128)} %param.13) | copy-start | bytes 1540
  24.9 39.0 %all-to-all-start = ((bf16[512,12,256]{2,0,1:T(8,128)(2,1)}), bf16[512,12,256]{2,0,1:T(8,128)(2,1)S(1)}, u32[]{:S(2)}, u32[]{:S(2)}) async-start(bf16[512,12,256]{2,0,1:T(8,128)(2,1)} %param.8), calls=%async_computation | async-start | bytes 6291456 | tf_op jit(solution)/shard_map/all_to_all | solution.py:78
  32.1 6.3 %copy-start.1 = (f32[512,128]{1,0:T(8,128)S(1)}, f32[512,128]{1,0:T(8,128)}, u32[]{:S(2)}) copy-start(f32[512,128]{1,0:T(8,128)} %param.7) | copy-start | bytes 786436
  73.3 3.8 %copy-start.4 = (f32[512,512]{1,0:T(8,128)S(1)}, f32[512,512]{1,0:T(8,128)}, u32[]{:S(2)}) copy-start(f32[512,512]{1,0:T(8,128)} %copy.30) | copy-start | bytes 3145732
  73.3 3.8 %copy-start.7 = (bf16[512,512,1]{1,0,2:T(8,128)(2,1)S(1)}, bf16[512,512,1]{1,0,2:T(8,128)(2,1)}, u32[]{:S(2)}) copy-start(bf16[512,512,1]{1,0,2:T(8,128)(2,1)} %reshape.38) | copy-start | bytes 1572868
  79.2 2.1 %copy-start.6 = (bf16[512,2,256]{0,2,1:T(8,128)(2,1)S(1)}, bf16[512,2,256]{0,2,1:T(8,128)(2,1)}, u32[]{:S(2)}) copy-start(bf16[512,2,256]{0,2,1:T(8,128)(2,1)} %copy.36) | copy-start | bytes 1572868
  81.3 2.1 %copy-start.5 = (f32[128,2,256]{0,2,1:T(8,128)S(1)}, f32[128,2,256]{0,2,1:T(8,128)}, u32[]{:S(2)}) copy-start(f32[128,2,256]{0,2,1:T(8,128)} %get-tuple-element.7) | copy-start | bytes 786436
  85.2 10.6 %all-to-all-start.3 = ((bf16[2,512,128]{2,1,0:T(8,128)(2,1)}), bf16[2,512,128]{2,1,0:T(8,128)(2,1)}, u32[]{:S(2)}, u32[]{:S(2)}) async-start(bf16[2,512,128]{2,1,0:T(8,128)(2,1)} %broadcast_in_dim.16), calls=%async_computation.3 | async-start | bytes 524288 | tf_op jit(solution)/shard_map/all_to_all | solution.py:20
  94.8 10.2 %copy-start.8 = (f32[512]{0:T(512)S(1)}, f32[512]{0:T(512)}, u32[]{:S(2)}) copy-start(f32[512]{0:T(512)} %param.9) | copy-start | bytes 6148
  95.8 20.0 %all-to-all-start.5 = ((bf16[2,256,6,256]{3,1,2,0:T(8,128)(2,1)}), bf16[2,256,6,256]{3,1,2,0:T(8,128)(2,1)S(1)}, u32[]{:S(2)}, u32[]{:S(2)}) async-start(bf16[2,256,6,256]{3,1,2,0:T(8,128)(2,1)} %get-tuple-element.5), calls=%async_computation.5 | async-start | bytes 3145728 | tf_op jit(solution)/shard_map/all_to_all | solution.py:55
  104.0 0.7 copy-start.2
  115.8 64.5 %all-to-all-start.4 = ((bf16[2,256,6,256]{3,1,2,0:T(8,128)(2,1)}), bf16[2,256,6,256]{3,1,2,0:T(8,128)(2,1)S(1)}, u32[]{:S(2)}, u32[]{:S(2)}) async-start(bf16[2,256,6,256]{3,1,2,0:T(8,128)(2,1)} %get-tuple-element.4), calls=%async_computation.4 | async-start | bytes 3145728 | tf_op jit(solution)/shard_map/all_to_all | solution.py:55
  123.4 45.9 %collective-permute-start = (f32[2,1,128]{2,1,0:T(1,128)S(1)}, f32[2,1,128]{2,1,0:T(1,128)S(1)}, u32[]{:S(2)}, u32[]{:S(2)}) collective-permute-start(f32[2,1,128]{2,1,0:T(1,128)S(1)} %pad_maximum_fusion.2), channel_id=1, source_target_pairs={{0,254},{2,0},{4,2},{6,4},{8,6},{10,8},{12,10},{14,12},{16,14},{18... | collective-permute-start | bytes 3080 | tf_op jit(solution)/shard_map/ppermute | solution.py:68
  170.5 0.7 copy-start.3
  171.2 7.2 %collective-permute-start.1 = (f32[1,128]{1,0:T(1,128)S(1)}, f32[1,128]{1,0:T(1,128)S(1)}, u32[]{:S(2)}, u32[]{:S(2)}) collective-permute-start(f32[1,128]{1,0:T(1,128)S(1)} %slice.33), channel_id=1, source_target_pairs={{0,2},{2,4},{4,6},{6,8},{8,10},{10,12},{12,14},{14,16},{16,18},{18... | collective-permute-start | bytes 1544 | tf_op jit(solution)/shard_map/ppermute | solution.py:68
where the time goes:
time: 183 us; the launch traced here: 182 us
  blocking collectives  58.8 us (32%)
  waiting for transfers between devices  35.4 us (19%)
  starting transfers between devices  35 us (19%)
  local copies, waits for them, and re-layouts  28.4 us (16%)
  matrix products  13.4 us (7%)
  other arithmetic  9.2 us (5%)
  between operations  2.04 us (1%)
    pmax x4, blocking collectives, by_axis(): array = lax.pmax(array, axis)  36.7 us
    all_to_all x2, blocking collectives, sent_to_all(): return lax.all_to_all(copies, axis, split_axis=0, concat_axis=0, tiled=True)  22.1 us
    all_to_all x1, waiting for transfers between devices, shards(): lax.all_to_all(micro_state, 'micro', split_axis=1, concat_axis=2, tiled=T...  18.7 us
    all_to_all x2, starting transfers between devices, cut_exchange(): lax.all_to_all(section, axis, split_axis=0, concat_axis=0, tiled=True)  14.1 us
    dot_general x4, matrix products, shards(): jnp.dot(micro_now.reshape(-1, width), coupling, preferred_element_type=jn...  10 us
    all_to_all x2, waiting for transfers between devices, cut_exchange(): lax.all_to_all(section, axis, split_axis=0, concat_axis=0, tiled=True)  9.21 us
    all_to_all x1, starting transfers between devices, sent_to_all(): return lax.all_to_all(copies, axis, split_axis=0, concat_axis=0, tiled=True)  7.32 us
    all_to_all x1, starting transfers between devices, shards(): lax.all_to_all(micro_state, 'micro', split_axis=1, concat_axis=2, tiled=T...  7.27 us
  transfers between devices with their start and end apart: 6, of which 4 were waited for; matrix products, arithmetic and copies ran while one was open for 13% of the time, Pallas kernels for 0%

commit v1 on v0

v1 whole, which is shorter than its diff:
```python
import functools

import jax
import jax.numpy as jnp
from jax import lax
from jax.experimental import pallas as pl
from jax.experimental.pallas import tpu as pltpu
from jax.sharding import Mesh
from jax.sharding import PartitionSpec as P


S = 12
STEPS = 4
MACRO = ("macro_0", "macro_1", "macro_2", "macro_3")
GROUP = ("macro_0", "macro_2", "macro_3")
CHUNKS = (2, 4, 3, 2, 1)
GROUPS = ((0,), (1, 2), (3, 4))
HIGHEST = lax.Precision.HIGHEST
VM = pl.BlockSpec(memory_space=pltpu.VMEM)
ANY = pl.BlockSpec(memory_space=pl.ANY)
HBM = pl.BlockSpec(memory_space=pltpu.HBM)
VMEM_BYTES = 6 * 2**20
FIRST_BYTES = 64_500_000
REST_BYTES = 60_500_000


def call(body, outs, ins, specs=None, scratch=(), flops=0, aliases=None, out_specs=None, limit=None):
    size = sum(a.size * a.dtype.itemsize for a in ins)
    return pl.pallas_call(
        body,
        out_shape=outs,
        in_specs=specs or [VM] * len(ins),
        out_specs=out_specs or jax.tree.map(lambda _: VM, outs),
        scratch_shapes=list(scratch),
        input_output_aliases=aliases or {},
        compiler_params=pltpu.CompilerParams(vmem_limit_bytes=limit or VMEM_BYTES),
        cost_estimate=pl.CostEstimate(flops=flops, bytes_accessed=size, transcendentals=0),
    )(*ins)


def f32dot(a, b, contract=((1,), (0,))):
    return lax.dot_general(a, b, (contract, ((), ())), precision=HIGHEST, preferred_element_type=jnp.float32)


def eighth():
    return (lax.axis_index("macro_2") % 4) * 2 + lax.axis_index("macro_3")


def slice_copies(plan, micro, outs, sems):
    me = lax.axis_index("micro")
    copies = []
    for k, ((start, mine), out) in enumerate(zip(plan, outs)):
        replicas, points, _ = out.shape
        at = (me if mine else 1 - me) * points
        where = micro.at[pl.ds(start, replicas), pl.ds(pl.multiple_of(at, points), points), :]
        copies.append(pltpu.make_async_copy(where, out, sems.at[k]))
    return copies


def cut_first(plan, micro, prop, fmap, readout, out, share, maps, sems, more):
    e = eighth()
    small = pl.ds(pl.multiple_of(e * 16, 16), 16)
    copies = slice_copies(plan, micro, [out], sems)
    copies += [
        pltpu.make_async_copy(fmap.at[small, :], maps.at[0], more.at[0]),
        pltpu.make_async_copy(readout.at[small, :], maps.at[1], more.at[1]),
        pltpu.make_async_copy(
            prop.at[pl.ds(pl.multiple_of(e * 64, 64), 64), :], share.at[pl.ds(0, 64), :], more.at[2]
        ),
    ]
    for copy in copies:
        copy.start()
    for copy in copies:
        copy.wait()
    for k in range(2):
        rows = maps[k]
        high = rows.astype(jnp.bfloat16)
        share[64 + 32 * k : 80 + 32 * k, :] = high
        share[80 + 32 * k : 96 + 32 * k, :] = (rows - high.astype(jnp.float32)).astype(jnp.bfloat16)


def cut_rest(plan, micro, _, *refs):
    copies = slice_copies(plan, micro, refs[:-1], refs[-1])
    for copy in copies:
        copy.start()
    for copy in copies:
        copy.wait()


def prepare(half, s0, s1, s2, s3, prop, fmap, macro, matrix_out, forcing_out, readout_out, far_map):
    me, e = lax.axis_index("micro"), eighth()
    points = forcing_out.shape[0]
    core, low_z, mid_z = e % 2, (e // 2) % 2, e // 4
    for k, pair in enumerate((s0, s1, s2, s3)):
        c = core if k % 2 == 0 else 1 - core
        z = low_z if k < 2 else 1 - low_z
        for t in range(2):
            share = pair.at[t]
            y = mid_z if t == 0 else 1 - mid_z
            y_row = (y + me) % 2
            spot = pl.ds(pl.multiple_of((y_row * 4 + z * 2 + c) * 64, 64), 64)
            matrix_out[spot, half:] = share[:64, :]
            at = pl.ds(pl.multiple_of((y * 4 + z * 2 + c) * 16, 16), 16)
            far_map[at, :] = share[64:80, :].astype(jnp.float32) + share[80:96, :].astype(jnp.float32)
            readout_out[at, :] = share[96:112, :].astype(jnp.float32) + share[112:128, :].astype(jnp.float32)
    matrix_out[:half, :half] = prop[pl.ds(pl.multiple_of(me * half, half), half), :]
    matrix_out[half:, :half] = prop[pl.ds(pl.multiple_of((1 - me) * half, half), half), :]
    mine = macro[pl.ds(pl.multiple_of(me * points, points), points), :]
    forcing_out[:, :half] = jnp.tanh(f32dot(mine, fmap[...]))
    forcing_out[:, half:] = jnp.tanh(f32dot(mine, far_map[...]))


def steps_of(start, at, micro, far, matrix, forcing, total_in, out, far_out, total_out, now, after, keep, sem):
    replicas, points, half = far.shape
    rows = replicas * points
    spot = pl.ds(pl.multiple_of(lax.axis_index("micro") * points, points), points)
    near = pltpu.make_async_copy(micro.at[pl.ds(start, replicas), spot, :], keep, sem.at[1])
    near.start()
    now[:, half:] = far[...].reshape(rows, half)
    near.wait()
    now[:, :half] = keep[...].reshape(rows, half)
    source, target = now, after
    copy = pltpu.make_async_copy(keep, out.at[pl.ds(start, replicas), spot, :], sem.at[0])
    for step in range(STEPS):
        for side in range(2):
            cols = slice(side * half, side * half + half)
            summed = jnp.dot(source[...], matrix[:, cols], preferred_element_type=jnp.float32)
            state = (summed.reshape(replicas, points, half) + forcing[:, cols][None]).astype(jnp.bfloat16)
            share = jnp.sum(jnp.tanh(state.astype(jnp.float32)), axis=0)
            if step > 0:
                share = total_out[:, cols] + share
            elif total_in is not None:
                share = total_in[:, cols] + share
            total_out[:, cols] = share
            if step < STEPS - 1:
                target[:, cols] = state.reshape(rows, half)
            elif side == 0:
                keep[...] = state
                copy.start()
            else:
                far_out[at : at + replicas] = state
        source, target = target, source
    return copy


def advance(start, at, inner, has_group, micro, far, matrix, forcing, *refs):
    total_in = refs[1] if inner else None
    out, far_out, total, now, after, keep, sem = refs[2 * inner + has_group :]
    copy = steps_of(start, at, micro, far, matrix, forcing, total_in, out, far_out, total, now, after, keep, sem)
    copy.wait()


def advance_last(start, at, has_group, micro, far, matrix, forcing, _, total_in, *refs):
    readout, far_readout, weights, velocity, macro, out, far_out, message, note = refs[has_group : has_group + 9]
    total, now, after, keep, sem = refs[has_group + 9 :]
    copy = steps_of(start, at, micro, far, matrix, forcing, total_in, out, far_out, total, now, after, keep, sem)
    points, half = far.shape[1:]
    me = lax.axis_index("micro")
    averaged = total[...] / (STEPS * S)
    forces = f32dot(averaged[:, :half], readout[...], ((1,), (1,)))
    forces = forces + f32dot(averaged[:, half:], far_readout[...], ((1,), (1,)))
    forces = forces.astype(jnp.bfloat16)
    message[:points, :] = forces
    drive = f32dot(forces.astype(jnp.float32), weights[...])
    base = velocity[pl.ds(pl.multiple_of(me * points, points), points), :]
    speeds = base * (1.5 + jnp.tanh(drive))
    row = lax.broadcasted_iota(jnp.int32, (8, speeds.shape[1]), 0)
    top = jnp.max(speeds, axis=0, keepdims=True)
    values = jnp.where(row == 0, top, jnp.where(row == 1, speeds[:1, :], speeds[points - 1 :, :]))
    count = macro.shape[0]
    note[...] = jnp.where(row == 3, macro[:1, :], jnp.where(row == 4, macro[count - 1 :, :], values))
    for k in range(3):
        piece = values.astype(jnp.bfloat16)
        message[points + 16 * k : points + 8 + 16 * k, :] = piece
        values = values - piece.astype(jnp.float32)
    copy.wait()


def group_spot(sizes, index):
    _, xs, zs, cs = sizes
    y = index // (cs * zs * xs)
    return (y * zs + (index // cs) % zs) * cs + index % cs, (index // (cs * zs)) % xs


def combine(sizes, own, across, beside, both, out):
    ys, xs, zs, cs = sizes
    me = lax.axis_index("micro")
    y, low, z, core = (lax.axis_index(name) for name in MACRO)
    first, zero = me == 0, low == 0
    off = across.shape[0] - 48
    parts = [across[off + 16 * k : off + 8 + 16 * k, :].astype(jnp.float32) for k in range(3)]
    far = parts[0] + parts[1] + parts[2]
    a, c, d = ([ref[k : k + 1, :] for k in range(3)] for ref in (own, beside, both))
    b = [far[k : k + 1, :] for k in range(3)]
    top = jnp.maximum(jnp.maximum(a[0], b[0]), jnp.maximum(c[0], d[0]))
    mine = (jnp.where(first, a[1], b[1]), jnp.where(first, b[2], a[2]))
    other = (jnp.where(first, c[1], d[1]), jnp.where(first, d[2], c[2]))
    block0 = [jnp.where(zero, x, v) for x, v in zip(mine, other)]
    block1 = [jnp.where(zero, v, x) for x, v in zip(mine, other)]
    lane = lax.broadcasted_iota(jnp.int32, top.shape, 1)
    value = top
    for k, v in enumerate(block0 + block1):
        value = jnp.where(lane == k + 1, v, value)
    total = ys * xs * zs * cs
    up = (z == zs - 1) & (core == cs - 1)
    down = (z == 0) & (core == 0)
    after_low = jnp.where(up, 1 - low, low)
    before_low = jnp.where(down, 1 - low, low)
    after_spot, _ = group_spot(sizes, (((y * xs + after_low) * zs + z) * cs + core + 1) % total)
    before_spot, _ = group_spot(sizes, (((y * xs + before_low) * zs + z) * cs + core + total - 1) % total)
    last_state = jnp.where(up, beside[4:5, :], own[4:5, :])
    first_state = jnp.where(down, beside[3:4, :], own[3:4, :])
    row = lax.broadcasted_iota(jnp.int32, out.shape, 0)
    rows = jnp.where(row % 2 == 0, value, 0.0)
    rows = jnp.where(row == 2 * after_spot + 1, last_state, rows)
    out[...] = jnp.where(row == 2 * before_spot + 1, first_state, rows)


def finish(sizes, table, own, across, macro, velocity, weights, out, forces, state, flux):
    me = lax.axis_index("micro")
    points = own.shape[0] - 48
    count = out.shape[0]
    forces[pl.ds(pl.multiple_of(me * points, points), points), :] = own[:points, :].astype(jnp.float32)
    forces[pl.ds(pl.multiple_of((1 - me) * points, points), points), :] = across[:points, :].astype(jnp.float32)
    values = table[...]
    row = lax.broadcasted_iota(jnp.int32, values.shape, 0)
    lane = lax.broadcasted_iota(jnp.int32, values.shape, 1)

    def pick(mask):
        kept = jnp.where(mask, values, -jnp.inf)
        return jnp.max(jnp.max(kept, axis=0, keepdims=True), axis=1, keepdims=True)

    ys, xs, zs, cs = sizes
    total = ys * xs * zs * cs
    spot = [lax.axis_index(name) for name in MACRO]
    here = ((spot[0] * xs + spot[1]) * zs + spot[2]) * cs + spot[3]
    prev_row, prev_low = group_spot(sizes, (here + total - 1) % total)
    next_row, next_low = group_spot(sizes, (here + 1) % total)
    fastest = pick((lane == 0) & (row % 2 == 0))
    prev_speed = pick((row == 2 * prev_row) & (lane == 2 + 2 * prev_low))
    next_speed = pick((row == 2 * next_row) & (lane == 1 + 2 * next_low))
    behind = table[pl.ds(2 * prev_row + 1, 1), :]
    ahead = table[pl.ds(2 * next_row + 1, 1), :]
    time_step = 0.8 / jnp.maximum(fastest, 1.0)
    speeds = velocity[...] * (1.5 + jnp.tanh(f32dot(forces[...], weights[...])))
    state[8 : 8 + count, :] = macro[...]
    flux[8 : 8 + count, :] = speeds * macro[...]
    state[7:8, :] = behind
    flux[7:8, :] = prev_speed * behind
    state[8 + count : 9 + count, :] = ahead
    flux[8 + count : 9 + count, :] = next_speed * ahead
    u0, u1, u2 = (state[k : k + count, :] for k in (7, 8, 9))
    f0, f1, f2 = (flux[k : k + count, :] for k in (7, 8, 9))
    high = 0.5 * (f1 + f2) - 0.5 * fastest * (u2 - u1)
    low = 0.5 * (f0 + f1) - 0.5 * fastest * (u1 - u0)
    out[...] = u1 - time_step * (high - low) + time_step * forces[...]


def place(start, array, _, out, sem):
    replicas, points, _ = array.shape
    spot = pl.ds(pl.multiple_of((1 - lax.axis_index("micro")) * points, points), points)
    copy = pltpu.make_async_copy(array, out.at[pl.ds(start, replicas), spot, :], sem.at[0])
    copy.start()
    copy.wait()


def placed_in(array, start, out):
    return call(
        functools.partial(place, start),
        jax.ShapeDtypeStruct(out.shape, out.dtype),
        [array, out],
        specs=[VM, HBM],
        out_specs=HBM,
        scratch=[pltpu.SemaphoreType.DMA((1,))],
        aliases={1: 0},
    )


def swapped(value):
    return lax.ppermute(value, "micro", [(0, 1), (1, 0)])


def near_copy(value, low_z, core):
    count = lax.axis_size("macro_2")
    spots = [(z, c) for z in range(count) for c in range(2)]
    pairs = [(z * 2 + c, (z ^ low_z) * 2 + (c ^ core)) for z, c in spots]
    return lax.ppermute(value, ("macro_2", "macro_3"), pairs)


def starts(sizes):
    return [sum(sizes[:k]) for k in range(len(sizes))]


def shards(macro_state, micro_state, velocity, propagator, forcing_map, readout, speed_weights):
    f32, bf16 = jnp.float32, jnp.bfloat16
    count, fields = macro_state.shape
    half = micro_state.shape[2]
    points = count // 2
    micro = jnp.transpose(micro_state, (1, 0, 2))

    begin = starts(CHUNKS)
    chunks = [jax.ShapeDtypeStruct((size, points, half), bf16) for size in CHUNKS]
    first, share = call(
        functools.partial(cut_first, ((0, False),)),
        (chunks[0], jax.ShapeDtypeStruct((128, half), bf16)),
        [micro, propagator, forcing_map, readout],
        specs=[HBM] * 4,
        scratch=[pltpu.VMEM((2, 16, half), f32), pltpu.SemaphoreType.DMA((1,)), pltpu.SemaphoreType.DMA((3,))],
        limit=FIRST_BYTES,
    )
    plan = tuple((at, False) for at in begin[1:])
    rest = call(
        functools.partial(cut_rest, plan),
        tuple(chunks[1:]),
        [micro, share],
        specs=[HBM, ANY],
        scratch=[pltpu.SemaphoreType.DMA((len(plan),))],
        limit=REST_BYTES,
    )
    arrived = []
    for value in [first, *rest]:
        arrived.append(swapped(value))
    share = swapped(share)
    other = near_copy(share, 2, 0)
    share = jnp.stack([share, other])
    shares = [share]
    for z, c in ((0, 1), (1, 0), (1, 1)):
        shares.append(near_copy(share, z, c))
    weights = jnp.broadcast_to(speed_weights[:, None], (fields, 128))
    speed_base = jnp.broadcast_to(velocity[:, None], (count, 128))
    sums = jax.ShapeDtypeStruct((points, 2 * half), f32)
    matrix, forcing, far_readout = call(
        functools.partial(prepare, half),
        (jax.ShapeDtypeStruct((2 * half, 2 * half), bf16), sums, jax.ShapeDtypeStruct(readout.shape, f32)),
        [*shares, propagator, forcing_map, macro_state],
        scratch=[pltpu.VMEM(forcing_map.shape, f32)],
        flops=10**8,
    )
    out_type = jax.ShapeDtypeStruct(micro.shape, bf16)
    far_parts = []
    out = total = None
    for members in GROUPS:
        size_of_group = sum(CHUNKS[k] for k in members)
        group, at = None, 0
        for k in members:
            size = CHUNKS[k]
            whole = jax.ShapeDtypeStruct((size_of_group, points, half), bf16)
            ins, specs, aliases = [micro, arrived[k], matrix, forcing], [HBM] + [VM] * 3, {}
            inner = out is not None
            if inner:
                aliases = {4: 0, 5: 2}
                ins += [out, total]
                specs += [HBM, VM]
            if group is not None:
                aliases[len(ins)] = 1
                ins.append(group)
                specs.append(VM)
            scratch = [pltpu.VMEM((size * points, 2 * half), bf16)] * 2
            scratch += [pltpu.VMEM((size, points, half), bf16), pltpu.SemaphoreType.DMA((2,))]
            work = 2 * STEPS * size * points * (2 * half) ** 2
            if k < len(CHUNKS) - 1:
                out, group, total = call(
                    functools.partial(advance, begin[k], at, inner, group is not None),
                    (out_type, whole, sums),
                    ins,
                    specs=specs,
                    out_specs=(HBM, VM, VM),
                    scratch=scratch,
                    flops=work,
                    aliases=aliases,
                )
            else:
                aliases.pop(5)
                out, group, message, note = call(
                    functools.partial(advance_last, begin[k], at, group is not None),
                    (
                        out_type,
                        whole,
                        jax.ShapeDtypeStruct((points + 48, 128), bf16),
                        jax.ShapeDtypeStruct((8, 128), f32),
                    ),
                    [*ins, readout, far_readout, weights, speed_base, macro_state],
                    specs=specs + [VM] * 5,
                    out_specs=(HBM, VM, VM, VM),
                    scratch=[pltpu.VMEM(sums.shape, f32), *scratch],
                    flops=work,
                    aliases=aliases,
                )
            at += size
        far_parts.append(group)

    across = swapped(message)
    beside = lax.ppermute(note, "macro_1", [(0, 1), (1, 0)])
    both = lax.ppermute(note, ("macro_1", "micro"), [(k, 3 - k) for k in range(4)])
    returned = []
    for value in far_parts:
        returned.append(swapped(value))
    group = lax.axis_size(GROUP)
    sizes = tuple(lax.axis_size(name) for name in MACRO)
    rows = call(
        functools.partial(combine, sizes), jax.ShapeDtypeStruct((2 * group, 128), f32), [note, across, beside, both]
    )
    table = lax.all_to_all(rows.reshape(group, 2, 128), GROUP, split_axis=0, concat_axis=0, tiled=True)
    table = table.reshape(2 * group, 128)
    macro_next = call(
        functools.partial(finish, sizes),
        jax.ShapeDtypeStruct((count, fields), f32),
        [table, message, across, macro_state, speed_base, weights],
        scratch=[pltpu.VMEM((count, 128), f32), pltpu.VMEM((count + 16, 128), f32), pltpu.VMEM((count + 16, 128), f32)],
    )
    for members, value in zip(GROUPS, returned):
        out = placed_in(value, begin[members[0]], out)
    return macro_next, jnp.transpose(out, (1, 0, 2))


def solution(mesh):
    torus = Mesh(
        mesh.devices.reshape(4, 2, 8, 2, mesh.shape["micro"]),
        ("macro_0", "macro_1", "macro_2", "macro_3", "micro"),
    )
    placed = (
        P(MACRO, None),
        P(MACRO, None, "micro"),
        P(MACRO),
        P(None, "micro"),
        P(None, "micro"),
        P(None, "micro"),
        P(),
    )
    return jax.shard_map(
        shards,
        mesh=torus,
        in_specs=placed,
        out_specs=(P(MACRO, None), P(MACRO, None, "micro")),
        check_vma=False,
    )
```

time: 183 us -> 122 us (0.67)
  the two profiles are of different devices: /device:TPU:4 before, /device:TPU:1 now
where the time goes in v1:
time: 122 us
  waiting for transfers between devices  53.7 us (44%)
  starting transfers between devices  41.9 us (34%)
  Pallas kernels  24.2 us (20%)
    ppermute x10, waiting for transfers between devices, swapped(): return lax.ppermute(value, 'micro', [(0, 1), (1, 0)])  28.3 us
    pallas_call x13, Pallas kernels, call(): pl.pallas_call(body, out_shape=outs, in_specs=specs or [VM] * len(ins), o...  24.2 us
    all_to_all x1, starting transfers between devices, shards(): lax.all_to_all(rows.reshape(group, 2, 128), GROUP, split_axis=0, concat_a...  16.4 us
    ppermute x10, starting transfers between devices, swapped(): return lax.ppermute(value, 'micro', [(0, 1), (1, 0)])  14.3 us
    ppermute x1, waiting for transfers between devices, shards(): beside = lax.ppermute(note, 'macro_1', [(0, 1), (1, 0)])  9.44 us
    ppermute x4, starting transfers between devices, near_copy(): return lax.ppermute(value, ('macro_2', 'macro_3'), pairs)  8.09 us
    all_to_all x1, waiting for transfers between devices, shards(): lax.all_to_all(rows.reshape(group, 2, 128), GROUP, split_axis=0, concat_a...  8.04 us
    ppermute x4, waiting for transfers between devices, near_copy(): return lax.ppermute(value, ('macro_2', 'macro_3'), pairs)  5.27 us
  transfers between devices with their start and end apart: 17, of which 9 were waited for; matrix products, arithmetic and copies ran while one was open for 0% of the time, Pallas kernels for 15%

profile of v1, /device:TPU:1, one launch (start us, length us, event | category | flops | bytes accessed | tf_op | source)
XLA Modules:
  0.0 121.8 jit_solution(13178612429482613001)
XLA Ops:
  0.7 1.8 %shard_map.86 = (bf16[2,256,256]{2,1,0:T(8,128)(2,1)}, bf16[128,256]{1,0:T(8,128)(2,1)}) custom-call(bf16[12,512,256]{2,1,0:T(8,128)(2,1)} %bitcast.6, bf16[512,256]{1,0:T(8,128)(2,1)} %prop.3, f32[128,256]{1,0:T(8,128)} %fmap.3, f32[128,256]{1,0:T(8,128)} %refs_1_.1), custom_call_target="tpu_custom_call" | custom-call | bytes 3670016 | tf_op jit(solution)/shard_map/pallas_call | solution.py:29
  2.5 3.6 %collective-permute-start.1 = (bf16[128,256]{1,0:T(8,128)(2,1)}, bf16[128,256]{1,0:T(8,128)(2,1)S(1)}, u32[]{:S(2)}, u32[]{:S(2)}) collective-permute-start(bf16[128,256]{1,0:T(8,128)(2,1)} %get-tuple-element.27._), channel_id=1, source_target_pairs={{0,1},{1,0},{2,3},{3,2},{4,5},{5,4},{6,7},{7,6},{8,9},{9,8},{10,11... | collective-permute-start | bytes 196616 | tf_op jit(solution)/shard_map/ppermute | solution.py:280
  6.1 2.4 %shard_map.87 = (bf16[4,256,256]{2,1,0:T(8,128)(2,1)}, bf16[3,256,256]{2,1,0:T(8,128)(2,1)}, bf16[2,256,256]{2,1,0:T(8,128)(2,1)}, bf16[1,256,256]{2,1,0:T(8,128)(2,1)}) custom-call(bf16[12,512,256]{2,1,0:T(8,128)(2,1)} %bitcast.7, bf16[128,256]{1,0:T(8,128)(2,1)} %get-tuple-element.27._), custom_call_target="tpu_custom_call" | custom-call | bytes 3211264 | tf_op jit(solution)/shard_map/pallas_call | solution.py:29
  8.8 3.2 %collective-permute-start.2 = (bf16[128,256]{1,0:T(8,128)(2,1)S(1)}, bf16[128,256]{1,0:T(8,128)(2,1)S(1)}, u32[]{:S(2)}, u32[]{:S(2)}) collective-permute-start(bf16[128,256]{1,0:T(8,128)(2,1)S(1)} %collective-permute-done.1), channel_id=1, source_target_pairs={{0,8},{2,10},{4,12},{6,14},{8,0},{10,2},{12,4},{14,6},{16,24},{18,... | collective-permute-start | bytes 196616 | tf_op jit(solution)/shard_map/ppermute | solution.py:287
  12.0 2.6 %collective-permute-start.9 = (bf16[2,256,256]{2,1,0:T(8,128)(2,1)}, bf16[2,256,256]{2,1,0:T(8,128)(2,1)S(1)}, u32[]{:S(2)}, u32[]{:S(2)}) collective-permute-start(bf16[2,256,256]{2,1,0:T(8,128)(2,1)} %get-tuple-element.34), channel_id=1, source_target_pairs={{0,1},{1,0},{2,3},{3,2},{4,5},{5,4},{6,7},{7,6},{8,9},{9,8},{10,11... | collective-permute-start | bytes 786440 | tf_op jit(solution)/shard_map/ppermute | solution.py:280
  14.6 3.2 %collective-permute-start.3 = (bf16[2,128,256]{2,1,0:T(8,128)(2,1)S(1)}, bf16[2,128,256]{2,1,0:T(8,128)(2,1)S(1)}, u32[]{:S(2)}, u32[]{:S(2)}) collective-permute-start(bf16[2,128,256]{2,1,0:T(8,128)(2,1)S(1)} %pad_maximum_fusion.s0), channel_id=1, source_target_pairs={{0,2},{2,0},{4,6},{6,4},{8,10},{10,8},{12,14},{14,12},{16,18},{18,... | collective-permute-start | bytes 393224 | tf_op jit(solution)/shard_map/ppermute | solution.py:287
  18.1 1.4 %collective-permute-start.5 = (bf16[2,128,256]{2,1,0:T(8,128)(2,1)S(1)}, bf16[2,128,256]{2,1,0:T(8,128)(2,1)S(1)}, u32[]{:S(2)}, u32[]{:S(2)}) collective-permute-start(bf16[2,128,256]{2,1,0:T(8,128)(2,1)S(1)} %pad_maximum_fusion.s0), channel_id=1, source_target_pairs={{0,6},{2,4},{4,2},{6,0},{8,14},{10,12},{12,10},{14,8},{16,22},{18,... | collective-permute-start | bytes 393224 | tf_op jit(solution)/shard_map/ppermute | solution.py:287
  19.5 1.3 %collective-permute-start.7 = (bf16[3,256,256]{2,1,0:T(8,128)(2,1)}, bf16[3,256,256]{2,1,0:T(8,128)(2,1)S(1)}, u32[]{:S(2)}, u32[]{:S(2)}) collective-permute-start(bf16[3,256,256]{2,1,0:T(8,128)(2,1)} %get-tuple-element.32), channel_id=1, source_target_pairs={{0,1},{1,0},{2,3},{3,2},{4,5},{5,4},{6,7},{7,6},{8,9},{9,8},{10,11... | collective-permute-start | bytes 1179656 | tf_op jit(solution)/shard_map/ppermute | solution.py:280
  20.8 1.9 %collective-permute-done.4.s2 = bf16[2,128,256]{2,1,0:T(8,128)(2,1)S(1)} collective-permute-done((bf16[2,128,256]{2,1,0:T(8,128)(2,1)S(1)}, bf16[2,128,256]{2,1,0:T(8,128)(2,1)S(1)}, u32[]{:S(2)}, u32[]{:S(2)}) %collective-permute-start.4) | collective-permute-done | bytes 131104 | tf_op jit(solution)/shard_map/ppermute | solution.py:287
  22.7 3.4 %collective-permute-done.5.s3 = bf16[2,128,256]{2,1,0:T(8,128)(2,1)S(1)} collective-permute-done((bf16[2,128,256]{2,1,0:T(8,128)(2,1)S(1)}, bf16[2,128,256]{2,1,0:T(8,128)(2,1)S(1)}, u32[]{:S(2)}, u32[]{:S(2)}) %collective-permute-start.5) | collective-permute-done | bytes 131104 | tf_op jit(solution)/shard_map/ppermute | solution.py:287
  26.1 0.7 shard_map.88
  26.8 1.7 %collective-permute-done.9.far = bf16[2,256,256]{2,1,0:T(8,128)(2,1)S(1)} collective-permute-done((bf16[2,256,256]{2,1,0:T(8,128)(2,1)}, bf16[2,256,256]{2,1,0:T(8,128)(2,1)S(1)}, u32[]{:S(2)}, u32[]{:S(2)}) %collective-permute-start.9) | collective-permute-done | bytes 262176 | tf_op jit(solution)/shard_map/ppermute | solution.py:280
  28.5 2.8 %shard_map.89 = (bf16[12,512,256]{2,1,0:T(8,128)(2,1)}, bf16[2,256,256]{2,1,0:T(8,128)(2,1)}, f32[256,512]{1,0:T(8,128)S(1)}) custom-call(bf16[12,512,256]{2,1,0:T(8,128)(2,1)S(1)} %bitcast.8, bf16[2,256,256]{2,1,0:T(8,128)(2,1)S(1)} %collective-permute-done.9.far, bf16[512,512]{1,0:T(8,128)(2,1)S(1)} %get-tuple-element.29.matrix, ...), custom_call_target="tpu_custom_call" | custom-call | flops 1073741824 | bytes 4456448 | tf_op jit(solution)/shard_map/pallas_call | solution.py:29
  31.3 3.5 %shard_map.90 = (bf16[12,512,256]{2,1,0:T(8,128)(2,1)}, bf16[7,256,256]{2,1,0:T(8,128)(2,1)S(1)}, f32[256,512]{1,0:T(8,128)S(1)}) custom-call(bf16[12,512,256]{2,1,0:T(8,128)(2,1)S(1)} %bitcast.9, bf16[4,256,256]{2,1,0:T(8,128)(2,1)S(1)} %collective-permute-done.8.far, ...), custom_call_target="tpu_custom_call", output_to_operand_aliasing={{0}: (4, {}), {2}: (5, {})} | custom-call | flops 2147483648 | bytes 8388608 | tf_op jit(solution)/shard_map/pallas_call | solution.py:29
  34.8 2.1 %collective-permute-done.7.far = bf16[3,256,256]{2,1,0:T(8,128)(2,1)S(1)} collective-permute-done((bf16[3,256,256]{2,1,0:T(8,128)(2,1)}, bf16[3,256,256]{2,1,0:T(8,128)(2,1)S(1)}, u32[]{:S(2)}, u32[]{:S(2)}) %collective-permute-start.7) | collective-permute-done | bytes 393248 | tf_op jit(solution)/shard_map/ppermute | solution.py:280
  36.9 3.0 %shard_map.91 = (bf16[12,512,256]{2,1,0:T(8,128)(2,1)}, bf16[7,256,256]{2,1,0:T(8,128)(2,1)S(1)}, f32[256,512]{1,0:T(8,128)S(1)}) custom-call(bf16[12,512,256]{2,1,0:T(8,128)(2,1)S(1)} %bitcast.10, bf16[3,256,256]{2,1,0:T(8,128)(2,1)S(1)} %collective-permute-done.7.far, ...), custom_call_target="tpu_custom_call", output_to_operand_aliasing={{0}: (4, {}), {2}: (5, {}), {1}: (6, {})} | custom-call | flops 1610612736 | bytes 9175040 | tf_op jit(solution)/shard_map/pallas_call | solution.py:29
  40.0 2.9 %collective-permute-start.6 = (bf16[2,256,256]{2,1,0:T(8,128)(2,1)S(1)}, bf16[2,256,256]{2,1,0:T(8,128)(2,1)S(1)}, u32[]{:S(2)}, u32[]{:S(2)}) collective-permute-start(bf16[2,256,256]{2,1,0:T(8,128)(2,1)S(1)} %copy-done.9), channel_id=1, source_target_pairs={{0,1},{1,0},{2,3},{3,2},{4,5},{5,4},{6,7},{7,6},{8,9},{9,8},{10,11... | collective-permute-start | bytes 786440 | tf_op jit(solution)/shard_map/ppermute | solution.py:280
  43.2 24.0 %collective-permute-done.6.far = bf16[2,256,256]{2,1,0:T(8,128)(2,1)S(1)} collective-permute-done((bf16[2,256,256]{2,1,0:T(8,128)(2,1)S(1)}, bf16[2,256,256]{2,1,0:T(8,128)(2,1)S(1)}, u32[]{:S(2)}, u32[]{:S(2)}) %collective-permute-start.6) | collective-permute-done | bytes 262176 | tf_op jit(solution)/shard_map/ppermute | solution.py:280
  67.2 2.2 %shard_map.92 = (bf16[12,512,256]{2,1,0:T(8,128)(2,1)}, bf16[3,256,256]{2,1,0:T(8,128)(2,1)S(1)}, f32[256,512]{1,0:T(8,128)S(1)}) custom-call(bf16[12,512,256]{2,1,0:T(8,128)(2,1)S(1)} %bitcast.11, bf16[2,256,256]{2,1,0:T(8,128)(2,1)S(1)} %collective-permute-done.6.far, ...), custom_call_target="tpu_custom_call", output_to_operand_aliasing={{0}: (4, {}), {2}: (5, {})} | custom-call | flops 1073741824 | bytes 8126464 | tf_op jit(solution)/shard_map/pallas_call | solution.py:29
  70.2 2.5 %shard_map.93 = (bf16[12,512,256]{2,1,0:T(8,128)(2,1)}, bf16[3,256,256]{2,1,0:T(8,128)(2,1)S(1)}, bf16[304,128]{1,0:T(8,128)(2,1)S(1)}, f32[8,128]{1,0:T(8,128)S(1)}) custom-call(bf16[12,512,256]{2,1,0:T(8,128)(2,1)S(1)} %bitcast.12, bf16[1,256,256]{2,1,0:T(8,128)(2,1)S(1)} %collective-permute-done.far, ...), custom_call_target="tpu_custom_call", output_to_operand_aliasing={{0}: (4, {}), {1}: (6, {})} | custom-call | flops 536870912 | bytes 9240576 | tf_op jit(solution)/shard_map/pallas_call | solution.py:29
  72.8 3.0 %collective-permute-start.15 = (bf16[2,256,256]{2,1,0:T(8,128)(2,1)}, bf16[2,256,256]{2,1,0:T(8,128)(2,1)}, u32[]{:S(2)}, u32[]{:S(2)}) collective-permute-start(bf16[2,256,256]{2,1,0:T(8,128)(2,1)} %get-tuple-element.50), channel_id=1, source_target_pairs={{0,1},{1,0},{2,3},{3,2},{4,5},{5,4},{6,7},{7,6},{8,9},{9,8},{10,11... | collective-permute-start | bytes 786440 | tf_op jit(solution)/shard_map/ppermute | solution.py:280
  76.5 1.3 %collective-permute-start.11 = (f32[8,128]{1,0:T(8,128)S(1)}, f32[8,128]{1,0:T(8,128)S(1)}, u32[]{:S(2)}, u32[]{:S(2)}) collective-permute-start(f32[8,128]{1,0:T(8,128)S(1)} %get-tuple-element.46.own), channel_id=1, source_target_pairs={{0,32},{32,0},{1,33},{33,1},{2,34},{34,2},{3,35},{35,3},{4,36},{36... | collective-permute-start | bytes 12296 | tf_op jit(solution)/shard_map/ppermute | solution.py:393
  77.9 9.4 %collective-permute-done.11.beside = f32[8,128]{1,0:T(8,128)S(1)} collective-permute-done((f32[8,128]{1,0:T(8,128)S(1)}, f32[8,128]{1,0:T(8,128)S(1)}, u32[]{:S(2)}, u32[]{:S(2)}) %collective-permute-start.11) | collective-permute-done | bytes 4128 | tf_op jit(solution)/shard_map/ppermute | solution.py:393
  87.3 1.8 %collective-permute-start.12 = (f32[8,128]{1,0:T(8,128)S(1)}, f32[8,128]{1,0:T(8,128)S(1)}, u32[]{:S(2)}, u32[]{:S(2)}) collective-permute-start(f32[8,128]{1,0:T(8,128)S(1)} %get-tuple-element.46.own), channel_id=1, source_target_pairs={{0,33},{1,32},{32,1},{33,0},{2,35},{3,34},{34,3},{35,2},{4,37},{5,... | collective-permute-start | bytes 12296 | tf_op jit(solution)/shard_map/ppermute | solution.py:394
  89.1 2.6 %collective-permute-done.12.both = f32[8,128]{1,0:T(8,128)S(1)} collective-permute-done((f32[8,128]{1,0:T(8,128)S(1)}, f32[8,128]{1,0:T(8,128)S(1)}, u32[]{:S(2)}, u32[]{:S(2)}) %collective-permute-start.12) | collective-permute-done | bytes 4128 | tf_op jit(solution)/shard_map/ppermute | solution.py:394
  91.8 0.7 shard_map.94
  92.5 16.4 %all-to-all-start = ((f32[64,2,128]{2,1,0:T(2,128)}), f32[64,2,128]{2,1,0:T(2,128)S(1)}, u32[]{:S(2)}, u32[]{:S(2)}) async-start(f32[64,2,128]{2,1,0:T(2,128)} %bitcast.3), calls=%async_computation | async-start | bytes 131072 | tf_op jit(solution)/shard_map/all_to_all | solution.py:403
  108.9 1.7 %shard_map.96._ = bf16[12,512,256]{2,1,0:T(8,128)(2,1)} custom-call(bf16[2,256,256]{2,1,0:T(8,128)(2,1)} %collective-permute-done.15.array, bf16[12,512,256]{2,1,0:T(8,128)(2,1)} %get-tuple-element.51._), custom_call_target="tpu_custom_call", output_to_operand_aliasing={{}: (1, {})} | custom-call | bytes 3407872 | tf_op jit(solution)/shard_map/pallas_call | solution.py:29
  110.6 8.0 %all-to-all-done = f32[64,2,128]{2,1,0:T(2,128)S(1)} async-done(((f32[64,2,128]{2,1,0:T(2,128)}), f32[64,2,128]{2,1,0:T(2,128)S(1)}, u32[]{:S(2)}, u32[]{:S(2)}) %all-to-all-start) | async-done | bytes 65568 | tf_op jit(solution)/shard_map/all_to_all | solution.py:403
  118.6 1.2 %shard_map.95 = f32[512,128]{1,0:T(8,128)} custom-call(f32[128,128]{1,0:T(8,128)S(1)} %bitcast.13, bf16[304,128]{1,0:T(8,128)(2,1)S(1)} %copy-done.6, bf16[304,128]{1,0:T(8,128)(2,1)S(1)} %collective-permute-done.10.across, f32[512,128]{1,0:T(8,128)S(1)} %copy-done.1, f32[512,128]{1,0:T(8,128)S(1)} %broadcast_in_dim.5.refs_4_.velocity, ...), custom_call_target="tpu_custom_call" | custom-call | bytes 811008 | tf_op jit(solution)/shard_map/pallas_call | solution.py:29
  119.9 0.9 shard_map.97._
  120.8 0.8 shard_map.98
  (40 shorter events, 2.6 us)
Async XLA Ops:
  0.6 25.5 %copy-start.1 = (f32[512,128]{1,0:T(8,128)S(1)}, f32[512,128]{1,0:T(8,128)}, u32[]{:S(2)}) copy-start(f32[512,128]{1,0:T(8,128)} %macro.3) | copy-start | bytes 786436
  0.6 25.5 %copy-start.2 = (bf16[512,256]{1,0:T(8,128)(2,1)S(1)}, bf16[512,256]{1,0:T(8,128)(2,1)}, u32[]{:S(2)}) copy-start(bf16[512,256]{1,0:T(8,128)(2,1)} %prop.3) | copy-start | bytes 786436
  0.6 25.4 %copy-start.4 = (f32[128,256]{1,0:T(8,128)S(1)}, f32[128,256]{1,0:T(8,128)}, u32[]{:S(2)}) copy-start(f32[128,256]{1,0:T(8,128)} %fmap.3) | copy-start | bytes 393220
  2.5 26.0 %copy-start = (bf16[512,12,256]{2,0,1:T(8,128)(2,1)S(1)}, bf16[512,12,256]{2,0,1:T(8,128)(2,1)}, u32[]{:S(2)}) copy-start(bf16[512,12,256]{2,0,1:T(8,128)(2,1)} %param.8) | copy-start | bytes 9437188
  2.5 6.3 %collective-permute-start.1 = (bf16[128,256]{1,0:T(8,128)(2,1)}, bf16[128,256]{1,0:T(8,128)(2,1)S(1)}, u32[]{:S(2)}, u32[]{:S(2)}) collective-permute-start(bf16[128,256]{1,0:T(8,128)(2,1)} %get-tuple-element.27._), channel_id=1, source_target_pairs={{0,1},{1,0},{2,3},{3,2},{4,5},{5,4},{6,7},{7,6},{8,9},{9,8},{10,11... | collective-permute-start | bytes 196616 | tf_op jit(solution)/shard_map/ppermute | solution.py:280
  8.5 22.7 %collective-permute-start.8 = (bf16[4,256,256]{2,1,0:T(8,128)(2,1)}, bf16[4,256,256]{2,1,0:T(8,128)(2,1)S(1)}, u32[]{:S(2)}, u32[]{:S(2)}) collective-permute-start(bf16[4,256,256]{2,1,0:T(8,128)(2,1)} %get-tuple-element.33), channel_id=1, source_target_pairs={{0,1},{1,0},{2,3},{3,2},{4,5},{5,4},{6,7},{7,6},{8,9},{9,8},{10,11... | collective-permute-start | bytes 1572872 | tf_op jit(solution)/shard_map/ppermute | solution.py:280
  8.8 5.8 %collective-permute-start.2 = (bf16[128,256]{1,0:T(8,128)(2,1)S(1)}, bf16[128,256]{1,0:T(8,128)(2,1)S(1)}, u32[]{:S(2)}, u32[]{:S(2)}) collective-permute-start(bf16[128,256]{1,0:T(8,128)(2,1)S(1)} %collective-permute-done.1), channel_id=1, source_target_pairs={{0,8},{2,10},{4,12},{6,14},{8,0},{10,2},{12,4},{14,6},{16,24},{18,... | collective-permute-start | bytes 196616 | tf_op jit(solution)/shard_map/ppermute | solution.py:287
  12.0 16.5 %collective-permute-start.9 = (bf16[2,256,256]{2,1,0:T(8,128)(2,1)}, bf16[2,256,256]{2,1,0:T(8,128)(2,1)S(1)}, u32[]{:S(2)}, u32[]{:S(2)}) collective-permute-start(bf16[2,256,256]{2,1,0:T(8,128)(2,1)} %get-tuple-element.34), channel_id=1, source_target_pairs={{0,1},{1,0},{2,3},{3,2},{4,5},{5,4},{6,7},{7,6},{8,9},{9,8},{10,11... | collective-permute-start | bytes 786440 | tf_op jit(solution)/shard_map/ppermute | solution.py:280
  14.6 4.9 %collective-permute-start.3 = (bf16[2,128,256]{2,1,0:T(8,128)(2,1)S(1)}, bf16[2,128,256]{2,1,0:T(8,128)(2,1)S(1)}, u32[]{:S(2)}, u32[]{:S(2)}) collective-permute-start(bf16[2,128,256]{2,1,0:T(8,128)(2,1)S(1)} %pad_maximum_fusion.s0), channel_id=1, source_target_pairs={{0,2},{2,0},{4,6},{6,4},{8,10},{10,8},{12,14},{14,12},{16,18},{18,... | collective-permute-start | bytes 393224 | tf_op jit(solution)/shard_map/ppermute | solution.py:287
  17.8 5.0 %collective-permute-start.4 = (bf16[2,128,256]{2,1,0:T(8,128)(2,1)S(1)}, bf16[2,128,256]{2,1,0:T(8,128)(2,1)S(1)}, u32[]{:S(2)}, u32[]{:S(2)}) collective-permute-start(bf16[2,128,256]{2,1,0:T(8,128)(2,1)S(1)} %pad_maximum_fusion.s0), channel_id=1, source_target_pairs={{0,4},{2,6},{4,0},{6,2},{8,12},{10,14},{12,8},{14,10},{16,20},{18,... | collective-permute-start | bytes 393224 | tf_op jit(solution)/shard_map/ppermute | solution.py:287
  18.1 8.0 %collective-permute-start.5 = (bf16[2,128,256]{2,1,0:T(8,128)(2,1)S(1)}, bf16[2,128,256]{2,1,0:T(8,128)(2,1)S(1)}, u32[]{:S(2)}, u32[]{:S(2)}) collective-permute-start(bf16[2,128,256]{2,1,0:T(8,128)(2,1)S(1)} %pad_maximum_fusion.s0), channel_id=1, source_target_pairs={{0,6},{2,4},{4,2},{6,0},{8,14},{10,12},{12,10},{14,8},{16,22},{18,... | collective-permute-start | bytes 393224 | tf_op jit(solution)/shard_map/ppermute | solution.py:287
  19.5 17.4 %collective-permute-start.7 = (bf16[3,256,256]{2,1,0:T(8,128)(2,1)}, bf16[3,256,256]{2,1,0:T(8,128)(2,1)S(1)}, u32[]{:S(2)}, u32[]{:S(2)}) collective-permute-start(bf16[3,256,256]{2,1,0:T(8,128)(2,1)} %get-tuple-element.32), channel_id=1, source_target_pairs={{0,1},{1,0},{2,3},{3,2},{4,5},{5,4},{6,7},{7,6},{8,9},{9,8},{10,11... | collective-permute-start | bytes 1179656 | tf_op jit(solution)/shard_map/ppermute | solution.py:280
  36.9 3.1 %copy-start.9 = (bf16[2,256,256]{2,1,0:T(8,128)(2,1)S(1)}, bf16[2,256,256]{2,1,0:T(8,128)(2,1)}, u32[]{:S(2)}) copy-start(bf16[2,256,256]{2,1,0:T(8,128)(2,1)} %get-tuple-element.31) | copy-start | bytes 786436
  36.9 6.1 %copy-start.10 = (bf16[1,256,256]{2,1,0:T(8,128)(2,1)S(1)}, bf16[1,256,256]{2,1,0:T(8,128)(2,1)}, u32[]{:S(2)}) copy-start(bf16[1,256,256]{2,1,0:T(8,128)(2,1)} %get-tuple-element.28) | copy-start | bytes 393220
  39.9 80.0 %collective-permute-start.14 = (bf16[7,256,256]{2,1,0:T(8,128)(2,1)S(1)}, bf16[7,256,256]{2,1,0:T(8,128)(2,1)S(1)}, u32[]{:S(2)}, u32[]{:S(2)}) collective-permute-start(bf16[7,256,256]{2,1,0:T(8,128)(2,1)S(1)} %get-tuple-element.49), channel_id=1, source_target_pairs={{0,1},{1,0},{2,3},{3,2},{4,5},{5,4},{6,7},{7,6},{8,9},{9,8},{10,11... | collective-permute-start | bytes 2752520 | tf_op jit(solution)/shard_map/ppermute | solution.py:280
  40.0 27.2 %collective-permute-start.6 = (bf16[2,256,256]{2,1,0:T(8,128)(2,1)S(1)}, bf16[2,256,256]{2,1,0:T(8,128)(2,1)S(1)}, u32[]{:S(2)}, u32[]{:S(2)}) collective-permute-start(bf16[2,256,256]{2,1,0:T(8,128)(2,1)S(1)} %copy-done.9), channel_id=1, source_target_pairs={{0,1},{1,0},{2,3},{3,2},{4,5},{5,4},{6,7},{7,6},{8,9},{9,8},{10,11... | collective-permute-start | bytes 786440 | tf_op jit(solution)/shard_map/ppermute | solution.py:280
  43.0 27.1 %collective-permute-start = (bf16[1,256,256]{2,1,0:T(8,128)(2,1)S(1)}, bf16[1,256,256]{2,1,0:T(8,128)(2,1)S(1)}, u32[]{:S(2)}, u32[]{:S(2)}) collective-permute-start(bf16[1,256,256]{2,1,0:T(8,128)(2,1)S(1)} %copy-done.10), channel_id=1, source_target_pairs={{0,1},{1,0},{2,3},{3,2},{4,5},{5,4},{6,7},{7,6},{8,9},{9,8},{10,11... | collective-permute-start | bytes 393224 | tf_op jit(solution)/shard_map/ppermute | solution.py:280
  67.2 2.8 %copy-start.8 = (f32[128]{0:T(128)S(1)}, f32[128]{0:T(128)}, u32[]{:S(2)}) copy-start(f32[128]{0:T(128)} %param.13) | copy-start | bytes 1540
  67.2 2.9 %copy-start.7 = (f32[512]{0:T(512)S(1)}, f32[512]{0:T(512)}, u32[]{:S(2)}) copy-start(f32[512]{0:T(512)} %param.9) | copy-start | bytes 6148
  67.2 3.0 %copy-start.3 = (f32[128,256]{1,0:T(8,128)S(1)}, f32[128,256]{1,0:T(8,128)}, u32[]{:S(2)}) copy-start(f32[128,256]{1,0:T(8,128)} %refs_1_.1) | copy-start | bytes 393220
  72.7 48.1 %collective-permute-start.13 = (bf16[3,256,256]{2,1,0:T(8,128)(2,1)S(1)}, bf16[3,256,256]{2,1,0:T(8,128)(2,1)S(1)}, u32[]{:S(2)}, u32[]{:S(2)}) collective-permute-start(bf16[3,256,256]{2,1,0:T(8,128)(2,1)S(1)} %get-tuple-element.48), channel_id=1, source_target_pairs={{0,1},{1,0},{2,3},{3,2},{4,5},{5,4},{6,7},{7,6},{8,9},{9,8},{10,11... | collective-permute-start | bytes 1179656 | tf_op jit(solution)/shard_map/ppermute | solution.py:280
  72.8 36.0 %collective-permute-start.15 = (bf16[2,256,256]{2,1,0:T(8,128)(2,1)}, bf16[2,256,256]{2,1,0:T(8,128)(2,1)}, u32[]{:S(2)}, u32[]{:S(2)}) collective-permute-start(bf16[2,256,256]{2,1,0:T(8,128)(2,1)} %get-tuple-element.50), channel_id=1, source_target_pairs={{0,1},{1,0},{2,3},{3,2},{4,5},{5,4},{6,7},{7,6},{8,9},{9,8},{10,11... | collective-permute-start | bytes 786440 | tf_op jit(solution)/shard_map/ppermute | solution.py:280
  75.8 16.0 %collective-permute-start.10 = (bf16[304,128]{1,0:T(8,128)(2,1)S(1)}, bf16[304,128]{1,0:T(8,128)(2,1)S(1)}, u32[]{:S(2)}, u32[]{:S(2)}) collective-permute-start(bf16[304,128]{1,0:T(8,128)(2,1)S(1)} %get-tuple-element.47.own), channel_id=1, source_target_pairs={{0,1},{1,0},{2,3},{3,2},{4,5},{5,4},{6,7},{7,6},{8,9},{9,8},{10,11... | collective-permute-start | bytes 233480 | tf_op jit(solution)/shard_map/ppermute | solution.py:280
  75.9 0.6 copy-start.5
  76.5 10.8 %collective-permute-start.11 = (f32[8,128]{1,0:T(8,128)S(1)}, f32[8,128]{1,0:T(8,128)S(1)}, u32[]{:S(2)}, u32[]{:S(2)}) collective-permute-start(f32[8,128]{1,0:T(8,128)S(1)} %get-tuple-element.46.own), channel_id=1, source_target_pairs={{0,32},{32,0},{1,33},{33,1},{2,34},{34,2},{3,35},{35,3},{4,36},{36... | collective-permute-start | bytes 12296 | tf_op jit(solution)/shard_map/ppermute | solution.py:393
  87.3 4.5 %collective-permute-start.12 = (f32[8,128]{1,0:T(8,128)S(1)}, f32[8,128]{1,0:T(8,128)S(1)}, u32[]{:S(2)}, u32[]{:S(2)}) collective-permute-start(f32[8,128]{1,0:T(8,128)S(1)} %get-tuple-element.46.own), channel_id=1, source_target_pairs={{0,33},{1,32},{32,1},{33,0},{2,35},{3,34},{34,3},{35,2},{4,37},{5,... | collective-permute-start | bytes 12296 | tf_op jit(solution)/shard_map/ppermute | solution.py:394
  92.5 26.2 %all-to-all-start = ((f32[64,2,128]{2,1,0:T(2,128)}), f32[64,2,128]{2,1,0:T(2,128)S(1)}, u32[]{:S(2)}, u32[]{:S(2)}) async-start(f32[64,2,128]{2,1,0:T(2,128)} %bitcast.3), calls=%async_computation | async-start | bytes 131072 | tf_op jit(solution)/shard_map/all_to_all | solution.py:403
  108.9 9.8 %copy-start.6 = (bf16[304,128]{1,0:T(8,128)(2,1)S(1)}, bf16[304,128]{1,0:T(8,128)(2,1)}, u32[]{:S(2)}) copy-start(bf16[304,128]{1,0:T(8,128)(2,1)} %copy-done.5) | copy-start | bytes 233476

commit v2 on v1

--- a/solution.py
+++ b/solution.py
@@ -13,8 +13,10 @@
 STEPS = 4
 MACRO = ("macro_0", "macro_1", "macro_2", "macro_3")
 GROUP = ("macro_0", "macro_2", "macro_3")
-CHUNKS = (2, 4, 3, 2, 1)
-GROUPS = ((0,), (1, 2), (3, 4))
+CHUNKS = (1, 2, 5, 3, 1)
+UNITS = ((0, 1), (2,), (3,), (4,))
+GROUPS = ((0,), (1, 2, 3))
+SHARE = 128
 HIGHEST = lax.Precision.HIGHEST
 VM = pl.BlockSpec(memory_space=pltpu.VMEM)
 ANY = pl.BlockSpec(memory_space=pl.ANY)
@@ -57,15 +59,20 @@
     return copies
 
 
-def cut_first(plan, micro, prop, fmap, readout, out, share, maps, sems, more):
+def cut_first(replicas, points, micro, prop, fmap, readout, out, maps, sems, more):
     e = eighth()
+    base = replicas * points
     small = pl.ds(pl.multiple_of(e * 16, 16), 16)
-    copies = slice_copies(plan, micro, [out], sems)
+    spot = pl.ds(pl.multiple_of((1 - lax.axis_index("micro")) * points, points), points)
+    copies = [
+        pltpu.make_async_copy(micro.at[k, spot, :], out.at[pl.ds(k * points, points), :], sems.at[k])
+        for k in range(replicas)
+    ]
     copies += [
         pltpu.make_async_copy(fmap.at[small, :], maps.at[0], more.at[0]),
         pltpu.make_async_copy(readout.at[small, :], maps.at[1], more.at[1]),
         pltpu.make_async_copy(
-            prop.at[pl.ds(pl.multiple_of(e * 64, 64), 64), :], share.at[pl.ds(0, 64), :], more.at[2]
+            prop.at[pl.ds(pl.multiple_of(e * 64, 64), 64), :], out.at[pl.ds(base, 64), :], more.at[2]
         ),
     ]
     for copy in copies:
@@ -75,8 +82,9 @@
     for k in range(2):
         rows = maps[k]
         high = rows.astype(jnp.bfloat16)
-        share[64 + 32 * k : 80 + 32 * k, :] = high
-        share[80 + 32 * k : 96 + 32 * k, :] = (rows - high.astype(jnp.float32)).astype(jnp.bfloat16)
+        at = base + 64 + 32 * k
+        out[at : at + 16, :] = high
+        out[at + 16 : at + 32, :] = (rows - high.astype(jnp.float32)).astype(jnp.bfloat16)
 
 
 def cut_rest(plan, micro, _, *refs):
@@ -110,13 +118,18 @@
     forcing_out[:, half:] = jnp.tanh(f32dot(mine, far_map[...]))
 
 
-def steps_of(start, at, micro, far, matrix, forcing, total_in, out, far_out, total_out, now, after, keep, sem):
-    replicas, points, half = far.shape
+def steps_of(start, at, micro, fars, matrix, forcing, total_in, out, far_out, total_out, now, after, keep, sem):
+    points, half = far_out.shape[1:]
+    replicas = keep.shape[0]
     rows = replicas * points
     spot = pl.ds(pl.multiple_of(lax.axis_index("micro") * points, points), points)
     near = pltpu.make_async_copy(micro.at[pl.ds(start, replicas), spot, :], keep, sem.at[1])
     near.start()
-    now[:, half:] = far[...].reshape(rows, half)
+    row = 0
+    for far in fars:
+        count = far.shape[0] * points if len(far.shape) == 3 else far.shape[0] - SHARE
+        now[row : row + count, half:] = far[:count, :] if len(far.shape) == 2 else far[...].reshape(count, half)
+        row += count
     near.wait()
     now[:, :half] = keep[...].reshape(rows, half)
     source, target = now, after
@@ -143,27 +156,38 @@
     return copy
 
 
-def advance(start, at, inner, has_group, micro, far, matrix, forcing, *refs):
+def advance(start, at, parts, inner, has_group, micro, *refs):
+    fars, (matrix, forcing), refs = refs[:parts], refs[parts : parts + 2], refs[parts + 2 :]
     total_in = refs[1] if inner else None
     out, far_out, total, now, after, keep, sem = refs[2 * inner + has_group :]
-    copy = steps_of(start, at, micro, far, matrix, forcing, total_in, out, far_out, total, now, after, keep, sem)
+    copy = steps_of(start, at, micro, fars, matrix, forcing, total_in, out, far_out, total, now, after, keep, sem)
     copy.wait()
 
 
-def advance_last(start, at, has_group, micro, far, matrix, forcing, _, total_in, *refs):
-    readout, far_readout, weights, velocity, macro, out, far_out, message, note = refs[has_group : has_group + 9]
-    total, now, after, keep, sem = refs[has_group + 9 :]
-    copy = steps_of(start, at, micro, far, matrix, forcing, total_in, out, far_out, total, now, after, keep, sem)
-    points, half = far.shape[1:]
+def spread(row):
+    return jnp.broadcast_to(row, (row.shape[1], row.shape[1])).T
+
+
+def base_speeds(velocity, start, count):
+    return jnp.concatenate([spread(velocity[pl.ds(start + k, 1), :]) for k in range(count)], axis=0)
+
+
+def advance_last(start, at, parts, has_group, micro, *refs):
+    fars, (matrix, forcing), refs = refs[:parts], refs[parts : parts + 2], refs[parts + 3 :]
+    total_in, refs = refs[0], refs[1 + has_group :]
+    readout, far_readout, weights, velocity, macro, out, far_out, message, note = refs[:9]
+    total, now, after, keep, sem = refs[9:]
+    copy = steps_of(start, at, micro, fars, matrix, forcing, total_in, out, far_out, total, now, after, keep, sem)
+    points, half = far_out.shape[1:]
     me = lax.axis_index("micro")
     averaged = total[...] / (STEPS * S)
     forces = f32dot(averaged[:, :half], readout[...], ((1,), (1,)))
     forces = forces + f32dot(averaged[:, half:], far_readout[...], ((1,), (1,)))
     forces = forces.astype(jnp.bfloat16)
     message[:points, :] = forces
-    drive = f32dot(forces.astype(jnp.float32), weights[...])
-    base = velocity[pl.ds(pl.multiple_of(me * points, points), points), :]
-    speeds = base * (1.5 + jnp.tanh(drive))
+    drive = f32dot(forces.astype(jnp.float32), spread(weights[...]))
+    blocks = points // 128
+    speeds = base_speeds(velocity, me * blocks, blocks) * (1.5 + jnp.tanh(drive))
     row = lax.broadcasted_iota(jnp.int32, (8, speeds.shape[1]), 0)
     top = jnp.max(speeds, axis=0, keepdims=True)
     values = jnp.where(row == 0, top, jnp.where(row == 1, speeds[:1, :], speeds[points - 1 :, :]))
@@ -216,12 +240,22 @@
     out[...] = jnp.where(row == 2 * before_spot + 1, first_state, rows)
 
 
-def finish(sizes, table, own, across, macro, velocity, weights, out, forces, state, flux):
+def before_finish(own, across, macro, velocity, weights, packed, forces, flux):
     me = lax.axis_index("micro")
     points = own.shape[0] - 48
-    count = out.shape[0]
+    count = macro.shape[0]
     forces[pl.ds(pl.multiple_of(me * points, points), points), :] = own[:points, :].astype(jnp.float32)
     forces[pl.ds(pl.multiple_of((1 - me) * points, points), points), :] = across[:points, :].astype(jnp.float32)
+    flux[:8, :] = jnp.zeros((8, flux.shape[1]), jnp.float32)
+    flux[8 + count :, :] = jnp.zeros((8, flux.shape[1]), jnp.float32)
+    base = base_speeds(velocity, 0, count // 128)
+    flux[8 : 8 + count, :] = base * (1.5 + jnp.tanh(f32dot(forces[...], spread(weights[...])))) * macro[...]
+    packed[:count, :] = macro[...]
+    packed[count:, :] = forces[...] - 0.5 * (flux[9 : 9 + count, :] - flux[7 : 7 + count, :])
+
+
+def finish(sizes, table, packed, out, state):
+    count = out.shape[0]
     values = table[...]
     row = lax.broadcasted_iota(jnp.int32, values.shape, 0)
     lane = lax.broadcasted_iota(jnp.int32, values.shape, 1)
@@ -242,18 +276,13 @@
     behind = table[pl.ds(2 * prev_row + 1, 1), :]
     ahead = table[pl.ds(2 * next_row + 1, 1), :]
     time_step = 0.8 / jnp.maximum(fastest, 1.0)
-    speeds = velocity[...] * (1.5 + jnp.tanh(f32dot(forces[...], weights[...])))
-    state[8 : 8 + count, :] = macro[...]
-    flux[8 : 8 + count, :] = speeds * macro[...]
+    state[8 : 8 + count, :] = packed[:count, :]
     state[7:8, :] = behind
-    flux[7:8, :] = prev_speed * behind
     state[8 + count : 9 + count, :] = ahead
-    flux[8 + count : 9 + count, :] = next_speed * ahead
     u0, u1, u2 = (state[k : k + count, :] for k in (7, 8, 9))
-    f0, f1, f2 = (flux[k : k + count, :] for k in (7, 8, 9))
-    high = 0.5 * (f1 + f2) - 0.5 * fastest * (u2 - u1)
-    low = 0.5 * (f0 + f1) - 0.5 * fastest * (u1 - u0)
-    out[...] = u1 - time_step * (high - low) + time_step * forces[...]
+    out[...] = u1 + time_step * (packed[count:, :] + 0.5 * fastest * ((u2 - u1) - (u1 - u0)))
+    out[:1, :] = out[:1, :] + 0.5 * time_step * (prev_speed * behind)
+    out[count - 1 :, :] = out[count - 1 :, :] - 0.5 * time_step * (next_speed * ahead)
 
 
 def place(start, array, _, out, sem):
@@ -300,19 +329,23 @@
 
     begin = starts(CHUNKS)
     chunks = [jax.ShapeDtypeStruct((size, points, half), bf16) for size in CHUNKS]
-    first, share = call(
-        functools.partial(cut_first, ((0, False),)),
-        (chunks[0], jax.ShapeDtypeStruct((128, half), bf16)),
+    first = call(
+        functools.partial(cut_first, CHUNKS[0], points),
+        jax.ShapeDtypeStruct((CHUNKS[0] * points + SHARE, half), bf16),
         [micro, propagator, forcing_map, readout],
         specs=[HBM] * 4,
-        scratch=[pltpu.VMEM((2, 16, half), f32), pltpu.SemaphoreType.DMA((1,)), pltpu.SemaphoreType.DMA((3,))],
+        scratch=[
+            pltpu.VMEM((2, 16, half), f32),
+            pltpu.SemaphoreType.DMA((CHUNKS[0],)),
+            pltpu.SemaphoreType.DMA((3,)),
+        ],
         limit=FIRST_BYTES,
     )
     plan = tuple((at, False) for at in begin[1:])
     rest = call(
         functools.partial(cut_rest, plan),
         tuple(chunks[1:]),
-        [micro, share],
+        [micro, first],
         specs=[HBM, ANY],
         scratch=[pltpu.SemaphoreType.DMA((len(plan),))],
         limit=REST_BYTES,
@@ -320,14 +353,14 @@
     arrived = []
     for value in [first, *rest]:
         arrived.append(swapped(value))
-    share = swapped(share)
+    share = arrived[0][CHUNKS[0] * points :]
     other = near_copy(share, 2, 0)
     share = jnp.stack([share, other])
     shares = [share]
     for z, c in ((0, 1), (1, 0), (1, 1)):
         shares.append(near_copy(share, z, c))
-    weights = jnp.broadcast_to(speed_weights[:, None], (fields, 128))
-    speed_base = jnp.broadcast_to(velocity[:, None], (count, 128))
+    weights = speed_weights.reshape(1, fields)
+    speed_base = velocity.reshape(count // 128, 128)
     sums = jax.ShapeDtypeStruct((points, 2 * half), f32)
     matrix, forcing, far_readout = call(
         functools.partial(prepare, half),
@@ -340,15 +373,17 @@
     far_parts = []
     out = total = None
     for members in GROUPS:
-        size_of_group = sum(CHUNKS[k] for k in members)
+        size_of_group = sum(CHUNKS[k] for u in members for k in UNITS[u])
         group, at = None, 0
-        for k in members:
-            size = CHUNKS[k]
+        for u in members:
+            parts, start = len(UNITS[u]), begin[UNITS[u][0]]
+            size = sum(CHUNKS[k] for k in UNITS[u])
             whole = jax.ShapeDtypeStruct((size_of_group, points, half), bf16)
-            ins, specs, aliases = [micro, arrived[k], matrix, forcing], [HBM] + [VM] * 3, {}
+            ins = [micro, *(arrived[k] for k in UNITS[u]), matrix, forcing]
+            specs, aliases = [HBM] + [VM] * (parts + 2), {}
             inner = out is not None
             if inner:
-                aliases = {4: 0, 5: 2}
+                aliases = {len(ins): 0, len(ins) + 1: 2}
                 ins += [out, total]
                 specs += [HBM, VM]
             if group is not None:
@@ -358,9 +393,9 @@
             scratch = [pltpu.VMEM((size * points, 2 * half), bf16)] * 2
             scratch += [pltpu.VMEM((size, points, half), bf16), pltpu.SemaphoreType.DMA((2,))]
             work = 2 * STEPS * size * points * (2 * half) ** 2
-            if k < len(CHUNKS) - 1:
+            if u < len(UNITS) - 1:
                 out, group, total = call(
-                    functools.partial(advance, begin[k], at, inner, group is not None),
+                    functools.partial(advance, start, at, parts, inner, group is not None),
                     (out_type, whole, sums),
                     ins,
                     specs=specs,
@@ -370,9 +405,9 @@
                     aliases=aliases,
                 )
             else:
-                aliases.pop(5)
+                aliases = {i: o for i, o in aliases.items() if o != 2}
                 out, group, message, note = call(
-                    functools.partial(advance_last, begin[k], at, group is not None),
+                    functools.partial(advance_last, start, at, parts, group is not None),
                     (
                         out_type,
                         whole,
@@ -402,14 +437,18 @@
     )
     table = lax.all_to_all(rows.reshape(group, 2, 128), GROUP, split_axis=0, concat_axis=0, tiled=True)
     table = table.reshape(2 * group, 128)
+    padded = pltpu.VMEM((count + 16, fields), f32)
+    packed = call(
+        before_finish,
+        jax.ShapeDtypeStruct((2 * count, fields), f32),
+        [message, across, macro_state, speed_base, weights],
+        scratch=[pltpu.VMEM((count, fields), f32), padded],
+    )
     macro_next = call(
-        functools.partial(finish, sizes),
-        jax.ShapeDtypeStruct((count, fields), f32),
-        [table, message, across, macro_state, speed_base, weights],
-        scratch=[pltpu.VMEM((count, 128), f32), pltpu.VMEM((count + 16, 128), f32), pltpu.VMEM((count + 16, 128), f32)],
+        functools.partial(finish, sizes), jax.ShapeDtypeStruct((count, fields), f32), [table, packed], scratch=[padded]
     )
     for members, value in zip(GROUPS, returned):
-        out = placed_in(value, begin[members[0]], out)
+        out = placed_in(value, begin[UNITS[members[0]][0]], out)
     return macro_next, jnp.transpose(out, (1, 0, 2))
 
 

time: 122 us -> 113 us (0.926)
  the two profiles are of different devices: /device:TPU:1 before, /device:TPU:4 now
where the time goes in v2:
time: 113 us; the launch traced here: 111 us
  waiting for transfers between devices  53.9 us (48%)
  starting transfers between devices  32.7 us (29%)
  Pallas kernels  22.8 us (20%)
    ppermute x1, waiting for transfers between devices, shards(): beside = lax.ppermute(note, 'macro_1', [(0, 1), (1, 0)])  28.5 us
    pallas_call x12, Pallas kernels, call(): pl.pallas_call(body, out_shape=outs, in_specs=specs or [VM] * len(ins), o...  22.8 us
    all_to_all x1, starting transfers between devices, shards(): lax.all_to_all(rows.reshape(group, 2, 128), GROUP, split_axis=0, concat_a...  12.6 us
    ppermute x8, starting transfers between devices, swapped(): return lax.ppermute(value, 'micro', [(0, 1), (1, 0)])  11.5 us
    ppermute x8, waiting for transfers between devices, swapped(): return lax.ppermute(value, 'micro', [(0, 1), (1, 0)])  9.63 us
    ppermute x4, waiting for transfers between devices, near_copy(): return lax.ppermute(value, ('macro_2', 'macro_3'), pairs)  7.53 us
    all_to_all x1, waiting for transfers between devices, shards(): lax.all_to_all(rows.reshape(group, 2, 128), GROUP, split_axis=0, concat_a...  7.51 us
    ppermute x4, starting transfers between devices, near_copy(): return lax.ppermute(value, ('macro_2', 'macro_3'), pairs)  5.47 us
  transfers between devices with their start and end apart: 15, of which 10 were waited for; matrix products, arithmetic and copies ran while one was open for 0% of the time, Pallas kernels for 16%

profile of v2, /device:TPU:4, one launch (start us, length us, event | category | flops | bytes accessed | tf_op | source)
XLA Modules:
  0.0 110.5 jit_solution(1551531988691303879)
XLA Ops:
  0.7 1.7 %shard_map.86._ = bf16[384,256]{1,0:T(8,128)(2,1)} custom-call(bf16[12,512,256]{2,1,0:T(8,128)(2,1)} %bitcast.9, bf16[512,256]{1,0:T(8,128)(2,1)} %prop.3, f32[128,256]{1,0:T(8,128)} %fmap.3, f32[128,256]{1,0:T(8,128)} %refs_6_.1), custom_call_target="tpu_custom_call" | custom-call | bytes 3670016 | tf_op jit(solution)/shard_map/pallas_call | solution.py:31
  2.4 2.3 %collective-permute-start.1 = (bf16[384,256]{1,0:T(8,128)(2,1)}, bf16[384,256]{1,0:T(8,128)(2,1)S(1)}, u32[]{:S(2)}, u32[]{:S(2)}) collective-permute-start(bf16[384,256]{1,0:T(8,128)(2,1)} %shard_map.86._), channel_id=1, source_target_pairs={{0,1},{1,0},{2,3},{3,2},{4,5},{5,4},{6,7},{7,6},{8,9},{9,8},{10,11... | collective-permute-start | bytes 589832 | tf_op jit(solution)/shard_map/ppermute | solution.py:309
  4.7 2.4 %shard_map.87 = (bf16[2,256,256]{2,1,0:T(8,128)(2,1)}, bf16[5,256,256]{2,1,0:T(8,128)(2,1)}, bf16[3,256,256]{2,1,0:T(8,128)(2,1)}, bf16[1,256,256]{2,1,0:T(8,128)(2,1)}) custom-call(bf16[12,512,256]{2,1,0:T(8,128)(2,1)} %bitcast.10, bf16[384,256]{1,0:T(8,128)(2,1)} %shard_map.86._), custom_call_target="tpu_custom_call" | custom-call | bytes 3342336 | tf_op jit(solution)/shard_map/pallas_call | solution.py:31
  7.1 1.4 %collective-permute-start.7 = (bf16[5,256,256]{2,1,0:T(8,128)(2,1)}, bf16[5,256,256]{2,1,0:T(8,128)(2,1)S(1)}, u32[]{:S(2)}, u32[]{:S(2)}) collective-permute-start(bf16[5,256,256]{2,1,0:T(8,128)(2,1)} %get-tuple-element.26), channel_id=1, source_target_pairs={{0,1},{1,0},{2,3},{3,2},{4,5},{5,4},{6,7},{7,6},{8,9},{9,8},{10,11... | collective-permute-start | bytes 1966088 | tf_op jit(solution)/shard_map/ppermute | solution.py:309
  8.5 3.4 %collective-permute-done.1.refs_0_ = bf16[384,256]{1,0:T(8,128)(2,1)S(1)} collective-permute-done((bf16[384,256]{1,0:T(8,128)(2,1)}, bf16[384,256]{1,0:T(8,128)(2,1)S(1)}, u32[]{:S(2)}, u32[]{:S(2)}) %collective-permute-start.1) | collective-permute-done | bytes 196640 | tf_op jit(solution)/shard_map/ppermute | solution.py:309
  12.0 3.4 %collective-permute-start.2 = (bf16[128,256]{1,0:T(8,128)(2,1)S(1)}, bf16[128,256]{1,0:T(8,128)(2,1)S(1)}, u32[]{:S(2)}, u32[]{:S(2)}) collective-permute-start(bf16[128,256]{1,0:T(8,128)(2,1)S(1)} %get-tuple-element.43), channel_id=1, source_target_pairs={{0,8},{2,10},{4,12},{6,14},{8,0},{10,2},{12,4},{14,6},{16,24},{18,... | collective-permute-start | bytes 196616 | tf_op jit(solution)/shard_map/ppermute | solution.py:316
  15.3 2.2 %collective-permute-done.2 = bf16[128,256]{1,0:T(8,128)(2,1)S(1)} collective-permute-done((bf16[128,256]{1,0:T(8,128)(2,1)S(1)}, bf16[128,256]{1,0:T(8,128)(2,1)S(1)}, u32[]{:S(2)}, u32[]{:S(2)}) %collective-permute-start.2) | collective-permute-done | bytes 65568 | tf_op jit(solution)/shard_map/ppermute | solution.py:316
  17.7 2.0 %collective-permute-start.4 = (bf16[2,128,256]{2,1,0:T(8,128)(2,1)S(1)}, bf16[2,128,256]{2,1,0:T(8,128)(2,1)S(1)}, u32[]{:S(2)}, u32[]{:S(2)}) collective-permute-start(bf16[2,128,256]{2,1,0:T(8,128)(2,1)S(1)} %pad_maximum_fusion.s0), channel_id=1, source_target_pairs={{0,4},{2,6},{4,0},{6,2},{8,12},{10,14},{12,8},{14,10},{16,20},{18,... | collective-permute-start | bytes 393224 | tf_op jit(solution)/shard_map/ppermute | solution.py:316
  19.7 3.3 %collective-permute-done.5.s3 = bf16[2,128,256]{2,1,0:T(8,128)(2,1)S(1)} collective-permute-done((bf16[2,128,256]{2,1,0:T(8,128)(2,1)S(1)}, bf16[2,128,256]{2,1,0:T(8,128)(2,1)S(1)}, u32[]{:S(2)}, u32[]{:S(2)}) %collective-permute-start.5) | collective-permute-done | bytes 131104 | tf_op jit(solution)/shard_map/ppermute | solution.py:316
  23.0 1.3 %collective-permute-start = (bf16[1,256,256]{2,1,0:T(8,128)(2,1)}, bf16[1,256,256]{2,1,0:T(8,128)(2,1)S(1)}, u32[]{:S(2)}, u32[]{:S(2)}) collective-permute-start(bf16[1,256,256]{2,1,0:T(8,128)(2,1)} %get-tuple-element.22), channel_id=1, source_target_pairs={{0,1},{1,0},{2,3},{3,2},{4,5},{5,4},{6,7},{7,6},{8,9},{9,8},{10,11... | collective-permute-start | bytes 393224 | tf_op jit(solution)/shard_map/ppermute | solution.py:309
  24.3 2.0 %collective-permute-done.4.s2 = bf16[2,128,256]{2,1,0:T(8,128)(2,1)S(1)} collective-permute-done((bf16[2,128,256]{2,1,0:T(8,128)(2,1)S(1)}, bf16[2,128,256]{2,1,0:T(8,128)(2,1)S(1)}, u32[]{:S(2)}, u32[]{:S(2)}) %collective-permute-start.4) | collective-permute-done | bytes 131104 | tf_op jit(solution)/shard_map/ppermute | solution.py:316
  26.3 1.3 %collective-permute-start.6 = (bf16[3,256,256]{2,1,0:T(8,128)(2,1)}, bf16[3,256,256]{2,1,0:T(8,128)(2,1)S(1)}, u32[]{:S(2)}, u32[]{:S(2)}) collective-permute-start(bf16[3,256,256]{2,1,0:T(8,128)(2,1)} %get-tuple-element.25), channel_id=1, source_target_pairs={{0,1},{1,0},{2,3},{3,2},{4,5},{5,4},{6,7},{7,6},{8,9},{9,8},{10,11... | collective-permute-start | bytes 1179656 | tf_op jit(solution)/shard_map/ppermute | solution.py:309
  27.6 0.7 shard_map.88
  28.3 3.9 %collective-permute-done.8.refs_1_ = bf16[2,256,256]{2,1,0:T(8,128)(2,1)S(1)} collective-permute-done((bf16[2,256,256]{2,1,0:T(8,128)(2,1)}, bf16[2,256,256]{2,1,0:T(8,128)(2,1)S(1)}, u32[]{:S(2)}, u32[]{:S(2)}) %collective-permute-start.8) | collective-permute-done | bytes 262176 | tf_op jit(solution)/shard_map/ppermute | solution.py:309
  32.2 3.6 %shard_map.89 = (bf16[12,512,256]{2,1,0:T(8,128)(2,1)}, bf16[3,256,256]{2,1,0:T(8,128)(2,1)}, f32[256,512]{1,0:T(8,128)S(1)}) custom-call(bf16[12,512,256]{2,1,0:T(8,128)(2,1)S(1)} %bitcast.11, bf16[384,256]{1,0:T(8,128)(2,1)S(1)} %collective-permute-done.1.refs_0_, bf16[2,256,256]{2,1,0:T(8,128)(2,1)S(1)} %collective-permute-done.8.refs_1_, ...), custom_call_target="tpu_custom_call" | custom-call | flops 1610612736 | bytes 4653056 | tf_op jit(solution)/shard_map/pallas_call | solution.py:31
  35.7 4.2 %shard_map.90 = (bf16[12,512,256]{2,1,0:T(8,128)(2,1)}, bf16[9,256,256]{2,1,0:T(8,128)(2,1)S(1)}, f32[256,512]{1,0:T(8,128)S(1)}) custom-call(bf16[12,512,256]{2,1,0:T(8,128)(2,1)S(1)} %bitcast.12, bf16[5,256,256]{2,1,0:T(8,128)(2,1)S(1)} %collective-permute-done.7.refs_0_, ...), custom_call_target="tpu_custom_call", output_to_operand_aliasing={{0}: (4, {}), {2}: (5, {})} | custom-call | flops 2684354560 | bytes 8519680 | tf_op jit(solution)/shard_map/pallas_call | solution.py:31
  39.9 1.8 %collective-permute-done.6.refs_0_ = bf16[3,256,256]{2,1,0:T(8,128)(2,1)S(1)} collective-permute-done((bf16[3,256,256]{2,1,0:T(8,128)(2,1)}, bf16[3,256,256]{2,1,0:T(8,128)(2,1)S(1)}, u32[]{:S(2)}, u32[]{:S(2)}) %collective-permute-start.6) | collective-permute-done | bytes 393248 | tf_op jit(solution)/shard_map/ppermute | solution.py:309
  41.7 3.0 %shard_map.91 = (bf16[12,512,256]{2,1,0:T(8,128)(2,1)}, bf16[9,256,256]{2,1,0:T(8,128)(2,1)S(1)}, f32[256,512]{1,0:T(8,128)S(1)}) custom-call(bf16[12,512,256]{2,1,0:T(8,128)(2,1)S(1)} %bitcast.13, bf16[3,256,256]{2,1,0:T(8,128)(2,1)S(1)} %collective-permute-done.6.refs_0_, ...), custom_call_target="tpu_custom_call", output_to_operand_aliasing={{0}: (4, {}), {2}: (5, {}), {1}: (6, {})} | custom-call | flops 1610612736 | bytes 9437184 | tf_op jit(solution)/shard_map/pallas_call | solution.py:31
  44.8 2.5 %shard_map.92 = (bf16[12,512,256]{2,1,0:T(8,128)(2,1)}, bf16[9,256,256]{2,1,0:T(8,128)(2,1)S(1)}, bf16[304,128]{1,0:T(8,128)(2,1)S(1)}, f32[8,128]{1,0:T(8,128)S(1)}) custom-call(bf16[12,512,256]{2,1,0:T(8,128)(2,1)S(1)} %bitcast.14, bf16[1,256,256]{2,1,0:T(8,128)(2,1)S(1)} %collective-permute-done.refs_0_, ...), custom_call_target="tpu_custom_call", output_to_operand_aliasing={{0}: (4, {}), {1}: (6, {})} | custom-call | flops 536870912 | bytes 9701888 | tf_op jit(solution)/shard_map/pallas_call | solution.py:31
  47.3 1.6 %collective-permute-start.12 = (bf16[9,256,256]{2,1,0:T(8,128)(2,1)S(1)}, bf16[9,256,256]{2,1,0:T(8,128)(2,1)S(1)}, u32[]{:S(2)}, u32[]{:S(2)}) collective-permute-start(bf16[9,256,256]{2,1,0:T(8,128)(2,1)S(1)} %get-tuple-element.39), channel_id=1, source_target_pairs={{0,1},{1,0},{2,3},{3,2},{4,5},{5,4},{6,7},{7,6},{8,9},{9,8},{10,11... | collective-permute-start | bytes 3538952 | tf_op jit(solution)/shard_map/ppermute | solution.py:309
  48.9 2.0 %collective-permute-start.13 = (bf16[3,256,256]{2,1,0:T(8,128)(2,1)}, bf16[3,256,256]{2,1,0:T(8,128)(2,1)}, u32[]{:S(2)}, u32[]{:S(2)}) collective-permute-start(bf16[3,256,256]{2,1,0:T(8,128)(2,1)} %get-tuple-element.40), channel_id=1, source_target_pairs={{0,1},{1,0},{2,3},{3,2},{4,5},{5,4},{6,7},{7,6},{8,9},{9,8},{10,11... | collective-permute-start | bytes 1179656 | tf_op jit(solution)/shard_map/ppermute | solution.py:309
  50.9 1.6 %collective-permute-start.9 = (bf16[304,128]{1,0:T(8,128)(2,1)S(1)}, bf16[304,128]{1,0:T(8,128)(2,1)S(1)}, u32[]{:S(2)}, u32[]{:S(2)}) collective-permute-start(bf16[304,128]{1,0:T(8,128)(2,1)S(1)} %get-tuple-element.38.own), channel_id=1, source_target_pairs={{0,1},{1,0},{2,3},{3,2},{4,5},{5,4},{6,7},{7,6},{8,9},{9,8},{10,11... | collective-permute-start | bytes 233480 | tf_op jit(solution)/shard_map/ppermute | solution.py:309
  52.5 1.1 %collective-permute-start.11 = (f32[8,128]{1,0:T(8,128)S(1)}, f32[8,128]{1,0:T(8,128)S(1)}, u32[]{:S(2)}, u32[]{:S(2)}) collective-permute-start(f32[8,128]{1,0:T(8,128)S(1)} %get-tuple-element.37.own), channel_id=1, source_target_pairs={{0,33},{1,32},{32,1},{33,0},{2,35},{3,34},{34,3},{35,2},{4,37},{5,... | collective-permute-start | bytes 12296 | tf_op jit(solution)/shard_map/ppermute | solution.py:429
  53.6 2.0 %collective-permute-start.10 = (f32[8,128]{1,0:T(8,128)S(1)}, f32[8,128]{1,0:T(8,128)S(1)}, u32[]{:S(2)}, u32[]{:S(2)}) collective-permute-start(f32[8,128]{1,0:T(8,128)S(1)} %get-tuple-element.37.own), channel_id=1, source_target_pairs={{0,32},{32,0},{1,33},{33,1},{2,34},{34,2},{3,35},{35,3},{4,36},{36... | collective-permute-start | bytes 12296 | tf_op jit(solution)/shard_map/ppermute | solution.py:428
  55.6 0.8 collective-permute-done.11.both
  56.4 28.5 %collective-permute-done.10.beside = f32[8,128]{1,0:T(8,128)S(1)} collective-permute-done((f32[8,128]{1,0:T(8,128)S(1)}, f32[8,128]{1,0:T(8,128)S(1)}, u32[]{:S(2)}, u32[]{:S(2)}) %collective-permute-start.10) | collective-permute-done | bytes 4128 | tf_op jit(solution)/shard_map/ppermute | solution.py:428
  85.4 0.7 shard_map.93
  86.1 12.6 %all-to-all-start = ((f32[64,2,128]{2,1,0:T(2,128)}), f32[64,2,128]{2,1,0:T(2,128)S(1)}, u32[]{:S(2)}, u32[]{:S(2)}) async-start(f32[64,2,128]{2,1,0:T(2,128)} %bitcast.5), calls=%async_computation | async-start | bytes 131072 | tf_op jit(solution)/shard_map/all_to_all | solution.py:438
  99.2 1.8 %shard_map.96._ = bf16[12,512,256]{2,1,0:T(8,128)(2,1)} custom-call(bf16[3,256,256]{2,1,0:T(8,128)(2,1)} %collective-permute-done.13.array, bf16[12,512,256]{2,1,0:T(8,128)(2,1)} %get-tuple-element.41._), custom_call_target="tpu_custom_call", output_to_operand_aliasing={{}: (1, {})} | custom-call | bytes 3538944 | tf_op jit(solution)/shard_map/pallas_call | solution.py:31
  100.9 7.5 %all-to-all-done = f32[64,2,128]{2,1,0:T(2,128)S(1)} async-done(((f32[64,2,128]{2,1,0:T(2,128)}), f32[64,2,128]{2,1,0:T(2,128)S(1)}, u32[]{:S(2)}, u32[]{:S(2)}) %all-to-all-start) | async-done | bytes 65568 | tf_op jit(solution)/shard_map/all_to_all | solution.py:438
  108.4 0.9 shard_map.95
  109.4 1.0 shard_map.97
  (26 shorter events, 1.1 us)
Async XLA Ops:
  0.6 27.0 %copy-start.1 = (f32[512,128]{1,0:T(8,128)S(1)}, f32[512,128]{1,0:T(8,128)}, u32[]{:S(2)}) copy-start(f32[512,128]{1,0:T(8,128)} %macro.3) | copy-start | bytes 786436
  0.6 27.0 %copy-start.2 = (bf16[512,256]{1,0:T(8,128)(2,1)S(1)}, bf16[512,256]{1,0:T(8,128)(2,1)}, u32[]{:S(2)}) copy-start(bf16[512,256]{1,0:T(8,128)(2,1)} %prop.3) | copy-start | bytes 786436
  0.6 27.0 %copy-start.4 = (f32[128,256]{1,0:T(8,128)S(1)}, f32[128,256]{1,0:T(8,128)}, u32[]{:S(2)}) copy-start(f32[128,256]{1,0:T(8,128)} %fmap.3) | copy-start | bytes 393220
  2.4 29.8 %copy-start = (bf16[512,12,256]{2,0,1:T(8,128)(2,1)S(1)}, bf16[512,12,256]{2,0,1:T(8,128)(2,1)}, u32[]{:S(2)}) copy-start(bf16[512,12,256]{2,0,1:T(8,128)(2,1)} %param.8) | copy-start | bytes 9437188
  2.4 9.6 %collective-permute-start.1 = (bf16[384,256]{1,0:T(8,128)(2,1)}, bf16[384,256]{1,0:T(8,128)(2,1)S(1)}, u32[]{:S(2)}, u32[]{:S(2)}) collective-permute-start(bf16[384,256]{1,0:T(8,128)(2,1)} %shard_map.86._), channel_id=1, source_target_pairs={{0,1},{1,0},{2,3},{3,2},{4,5},{5,4},{6,7},{7,6},{8,9},{9,8},{10,11... | collective-permute-start | bytes 589832 | tf_op jit(solution)/shard_map/ppermute | solution.py:309
  7.1 28.6 %collective-permute-start.7 = (bf16[5,256,256]{2,1,0:T(8,128)(2,1)}, bf16[5,256,256]{2,1,0:T(8,128)(2,1)S(1)}, u32[]{:S(2)}, u32[]{:S(2)}) collective-permute-start(bf16[5,256,256]{2,1,0:T(8,128)(2,1)} %get-tuple-element.26), channel_id=1, source_target_pairs={{0,1},{1,0},{2,3},{3,2},{4,5},{5,4},{6,7},{7,6},{8,9},{9,8},{10,11... | collective-permute-start | bytes 1966088 | tf_op jit(solution)/shard_map/ppermute | solution.py:309
  12.0 5.6 %collective-permute-start.2 = (bf16[128,256]{1,0:T(8,128)(2,1)S(1)}, bf16[128,256]{1,0:T(8,128)(2,1)S(1)}, u32[]{:S(2)}, u32[]{:S(2)}) collective-permute-start(bf16[128,256]{1,0:T(8,128)(2,1)S(1)} %get-tuple-element.43), channel_id=1, source_target_pairs={{0,8},{2,10},{4,12},{6,14},{8,0},{10,2},{12,4},{14,6},{16,24},{18,... | collective-permute-start | bytes 196616 | tf_op jit(solution)/shard_map/ppermute | solution.py:316
  15.3 16.8 %collective-permute-start.8 = (bf16[2,256,256]{2,1,0:T(8,128)(2,1)}, bf16[2,256,256]{2,1,0:T(8,128)(2,1)S(1)}, u32[]{:S(2)}, u32[]{:S(2)}) collective-permute-start(bf16[2,256,256]{2,1,0:T(8,128)(2,1)} %get-tuple-element.27), channel_id=1, source_target_pairs={{0,1},{1,0},{2,3},{3,2},{4,5},{5,4},{6,7},{7,6},{8,9},{9,8},{10,11... | collective-permute-start | bytes 786440 | tf_op jit(solution)/shard_map/ppermute | solution.py:309
  17.6 5.4 %collective-permute-start.5 = (bf16[2,128,256]{2,1,0:T(8,128)(2,1)S(1)}, bf16[2,128,256]{2,1,0:T(8,128)(2,1)S(1)}, u32[]{:S(2)}, u32[]{:S(2)}) collective-permute-start(bf16[2,128,256]{2,1,0:T(8,128)(2,1)S(1)} %pad_maximum_fusion.s0), channel_id=1, source_target_pairs={{0,6},{2,4},{4,2},{6,0},{8,14},{10,12},{12,10},{14,8},{16,22},{18,... | collective-permute-start | bytes 393224 | tf_op jit(solution)/shard_map/ppermute | solution.py:316
  17.7 8.6 %collective-permute-start.4 = (bf16[2,128,256]{2,1,0:T(8,128)(2,1)S(1)}, bf16[2,128,256]{2,1,0:T(8,128)(2,1)S(1)}, u32[]{:S(2)}, u32[]{:S(2)}) collective-permute-start(bf16[2,128,256]{2,1,0:T(8,128)(2,1)S(1)} %pad_maximum_fusion.s0), channel_id=1, source_target_pairs={{0,4},{2,6},{4,0},{6,2},{8,12},{10,14},{12,8},{14,10},{16,20},{18,... | collective-permute-start | bytes 393224 | tf_op jit(solution)/shard_map/ppermute | solution.py:316
  19.7 7.9 %collective-permute-start.3 = (bf16[2,128,256]{2,1,0:T(8,128)(2,1)S(1)}, bf16[2,128,256]{2,1,0:T(8,128)(2,1)S(1)}, u32[]{:S(2)}, u32[]{:S(2)}) collective-permute-start(bf16[2,128,256]{2,1,0:T(8,128)(2,1)S(1)} %pad_maximum_fusion.s0), channel_id=1, source_target_pairs={{0,2},{2,0},{4,6},{6,4},{8,10},{10,8},{12,14},{14,12},{16,18},{18,... | collective-permute-start | bytes 393224 | tf_op jit(solution)/shard_map/ppermute | solution.py:316
  23.0 21.7 %collective-permute-start = (bf16[1,256,256]{2,1,0:T(8,128)(2,1)}, bf16[1,256,256]{2,1,0:T(8,128)(2,1)S(1)}, u32[]{:S(2)}, u32[]{:S(2)}) collective-permute-start(bf16[1,256,256]{2,1,0:T(8,128)(2,1)} %get-tuple-element.22), channel_id=1, source_target_pairs={{0,1},{1,0},{2,3},{3,2},{4,5},{5,4},{6,7},{7,6},{8,9},{9,8},{10,11... | collective-permute-start | bytes 393224 | tf_op jit(solution)/shard_map/ppermute | solution.py:309
  26.3 15.4 %collective-permute-start.6 = (bf16[3,256,256]{2,1,0:T(8,128)(2,1)}, bf16[3,256,256]{2,1,0:T(8,128)(2,1)S(1)}, u32[]{:S(2)}, u32[]{:S(2)}) collective-permute-start(bf16[3,256,256]{2,1,0:T(8,128)(2,1)} %get-tuple-element.25), channel_id=1, source_target_pairs={{0,1},{1,0},{2,3},{3,2},{4,5},{5,4},{6,7},{7,6},{8,9},{9,8},{10,11... | collective-permute-start | bytes 1179656 | tf_op jit(solution)/shard_map/ppermute | solution.py:309
  41.7 3.0 %copy-start.3 = (f32[128,256]{1,0:T(8,128)S(1)}, f32[128,256]{1,0:T(8,128)}, u32[]{:S(2)}) copy-start(f32[128,256]{1,0:T(8,128)} %refs_6_.1) | copy-start | bytes 393220
  41.7 3.0 %copy-start.5 = (f32[512]{0:T(512)S(1)}, f32[512]{0:T(512)}, u32[]{:S(2)}) copy-start(f32[512]{0:T(512)} %param.9) | copy-start | bytes 6148
  41.7 3.0 %copy-start.6 = (f32[128]{0:T(128)S(1)}, f32[128]{0:T(128)}, u32[]{:S(2)}) copy-start(f32[128]{0:T(128)} %param.13) | copy-start | bytes 1540
  47.3 62.1 %collective-permute-start.12 = (bf16[9,256,256]{2,1,0:T(8,128)(2,1)S(1)}, bf16[9,256,256]{2,1,0:T(8,128)(2,1)S(1)}, u32[]{:S(2)}, u32[]{:S(2)}) collective-permute-start(bf16[9,256,256]{2,1,0:T(8,128)(2,1)S(1)} %get-tuple-element.39), channel_id=1, source_target_pairs={{0,1},{1,0},{2,3},{3,2},{4,5},{5,4},{6,7},{7,6},{8,9},{9,8},{10,11... | collective-permute-start | bytes 3538952 | tf_op jit(solution)/shard_map/ppermute | solution.py:309
  48.9 50.2 %collective-permute-start.13 = (bf16[3,256,256]{2,1,0:T(8,128)(2,1)}, bf16[3,256,256]{2,1,0:T(8,128)(2,1)}, u32[]{:S(2)}, u32[]{:S(2)}) collective-permute-start(bf16[3,256,256]{2,1,0:T(8,128)(2,1)} %get-tuple-element.40), channel_id=1, source_target_pairs={{0,1},{1,0},{2,3},{3,2},{4,5},{5,4},{6,7},{7,6},{8,9},{9,8},{10,11... | collective-permute-start | bytes 1179656 | tf_op jit(solution)/shard_map/ppermute | solution.py:309
  50.9 34.5 %collective-permute-start.9 = (bf16[304,128]{1,0:T(8,128)(2,1)S(1)}, bf16[304,128]{1,0:T(8,128)(2,1)S(1)}, u32[]{:S(2)}, u32[]{:S(2)}) collective-permute-start(bf16[304,128]{1,0:T(8,128)(2,1)S(1)} %get-tuple-element.38.own), channel_id=1, source_target_pairs={{0,1},{1,0},{2,3},{3,2},{4,5},{5,4},{6,7},{7,6},{8,9},{9,8},{10,11... | collective-permute-start | bytes 233480 | tf_op jit(solution)/shard_map/ppermute | solution.py:309
  52.5 3.9 %collective-permute-start.11 = (f32[8,128]{1,0:T(8,128)S(1)}, f32[8,128]{1,0:T(8,128)S(1)}, u32[]{:S(2)}, u32[]{:S(2)}) collective-permute-start(f32[8,128]{1,0:T(8,128)S(1)} %get-tuple-element.37.own), channel_id=1, source_target_pairs={{0,33},{1,32},{32,1},{33,0},{2,35},{3,34},{34,3},{35,2},{4,37},{5,... | collective-permute-start | bytes 12296 | tf_op jit(solution)/shard_map/ppermute | solution.py:429
  53.6 31.3 %collective-permute-start.10 = (f32[8,128]{1,0:T(8,128)S(1)}, f32[8,128]{1,0:T(8,128)S(1)}, u32[]{:S(2)}, u32[]{:S(2)}) collective-permute-start(f32[8,128]{1,0:T(8,128)S(1)} %get-tuple-element.37.own), channel_id=1, source_target_pairs={{0,32},{32,0},{1,33},{33,1},{2,34},{34,2},{3,35},{35,3},{4,36},{36... | collective-permute-start | bytes 12296 | tf_op jit(solution)/shard_map/ppermute | solution.py:428
  86.1 22.4 %all-to-all-start = ((f32[64,2,128]{2,1,0:T(2,128)}), f32[64,2,128]{2,1,0:T(2,128)S(1)}, u32[]{:S(2)}, u32[]{:S(2)}) async-start(f32[64,2,128]{2,1,0:T(2,128)} %bitcast.5), calls=%async_computation | async-start | bytes 131072 | tf_op jit(solution)/shard_map/all_to_all | solution.py:438

commit v3 on v2

--- a/solution.py
+++ b/solution.py
@@ -22,7 +22,7 @@
 ANY = pl.BlockSpec(memory_space=pl.ANY)
 HBM = pl.BlockSpec(memory_space=pltpu.HBM)
 VMEM_BYTES = 6 * 2**20
-FIRST_BYTES = 64_500_000
+FIRST_BYTES = 66_800_000
 REST_BYTES = 60_500_000
 
 
@@ -193,10 +193,13 @@
     values = jnp.where(row == 0, top, jnp.where(row == 1, speeds[:1, :], speeds[points - 1 :, :]))
     count = macro.shape[0]
     note[...] = jnp.where(row == 3, macro[:1, :], jnp.where(row == 4, macro[count - 1 :, :], values))
-    for k in range(3):
-        piece = values.astype(jnp.bfloat16)
-        message[points + 16 * k : points + 8 + 16 * k, :] = piece
-        values = values - piece.astype(jnp.float32)
+    row = lax.broadcasted_iota(jnp.int32, (16, speeds.shape[1]), 0)
+    rest = jnp.where(row % 3 == 0, top, jnp.where(row % 3 == 1, speeds[:1, :], speeds[points - 1 :, :]))
+    parts = []
+    for _ in range(3):
+        parts.append(rest.astype(jnp.bfloat16).astype(jnp.float32))
+        rest = rest - parts[-1]
+    message[points:, :] = jnp.where(row < 3, parts[0], jnp.where(row < 6, parts[1], parts[2])).astype(jnp.bfloat16)
     copy.wait()
 
 
@@ -211,11 +214,9 @@
     me = lax.axis_index("micro")
     y, low, z, core = (lax.axis_index(name) for name in MACRO)
     first, zero = me == 0, low == 0
-    off = across.shape[0] - 48
-    parts = [across[off + 16 * k : off + 8 + 16 * k, :].astype(jnp.float32) for k in range(3)]
-    far = parts[0] + parts[1] + parts[2]
+    far = across[across.shape[0] - 16 :, :].astype(jnp.float32)
     a, c, d = ([ref[k : k + 1, :] for k in range(3)] for ref in (own, beside, both))
-    b = [far[k : k + 1, :] for k in range(3)]
+    b = [far[k : k + 1, :] + far[k + 3 : k + 4, :] + far[k + 6 : k + 7, :] for k in range(3)]
     top = jnp.maximum(jnp.maximum(a[0], b[0]), jnp.maximum(c[0], d[0]))
     mine = (jnp.where(first, a[1], b[1]), jnp.where(first, b[2], a[2]))
     other = (jnp.where(first, c[1], d[1]), jnp.where(first, d[2], c[2]))
@@ -242,7 +243,7 @@
 
 def before_finish(own, across, macro, velocity, weights, packed, forces, flux):
     me = lax.axis_index("micro")
-    points = own.shape[0] - 48
+    points = own.shape[0] - 16
     count = macro.shape[0]
     forces[pl.ds(pl.multiple_of(me * points, points), points), :] = own[:points, :].astype(jnp.float32)
     forces[pl.ds(pl.multiple_of((1 - me) * points, points), points), :] = across[:points, :].astype(jnp.float32)
@@ -285,12 +286,16 @@
     out[count - 1 :, :] = out[count - 1 :, :] - 0.5 * time_step * (next_speed * ahead)
 
 
-def place(start, array, _, out, sem):
+def place(start, array, _, out, sems):
     replicas, points, _ = array.shape
     spot = pl.ds(pl.multiple_of((1 - lax.axis_index("micro")) * points, points), points)
-    copy = pltpu.make_async_copy(array, out.at[pl.ds(start, replicas), spot, :], sem.at[0])
-    copy.start()
-    copy.wait()
+    copies = [
+        pltpu.make_async_copy(array.at[k], out.at[start + k, spot, :], sems.at[k]) for k in range(replicas)
+    ]
+    for copy in copies:
+        copy.start()
+    for copy in copies:
+        copy.wait()
 
 
 def placed_in(array, start, out):
@@ -300,7 +305,7 @@
         [array, out],
         specs=[VM, HBM],
         out_specs=HBM,
-        scratch=[pltpu.SemaphoreType.DMA((1,))],
+        scratch=[pltpu.SemaphoreType.DMA((array.shape[0],))],
         aliases={1: 0},
     )
 
@@ -411,7 +416,7 @@
                     (
                         out_type,
                         whole,
-                        jax.ShapeDtypeStruct((points + 48, 128), bf16),
+                        jax.ShapeDtypeStruct((points + 16, 128), bf16),
                         jax.ShapeDtypeStruct((8, 128), f32),
                     ),
                     [*ins, readout, far_readout, weights, speed_base, macro_state],

time: 113 us -> 112 us (level)
  no operation moved by 1% of the time
where the time goes in v3:
time: 112 us; the launch traced here: 110 us
  waiting for transfers between devices  53.8 us (48%)
  starting transfers between devices  32.7 us (29%)
  Pallas kernels  22.9 us (20%)
    ppermute x1, waiting for transfers between devices, shards(): beside = lax.ppermute(note, 'macro_1', [(0, 1), (1, 0)])  28.3 us
    pallas_call x12, Pallas kernels, call(): pl.pallas_call(body, out_shape=outs, in_specs=specs or [VM] * len(ins), o...  22.9 us
    all_to_all x1, starting transfers between devices, shards(): lax.all_to_all(rows.reshape(group, 2, 128), GROUP, split_axis=0, concat_a...  12.6 us
    ppermute x8, starting transfers between devices, swapped(): return lax.ppermute(value, 'micro', [(0, 1), (1, 0)])  11.4 us
    ppermute x8, waiting for transfers between devices, swapped(): return lax.ppermute(value, 'micro', [(0, 1), (1, 0)])  9.64 us
    ppermute x4, waiting for transfers between devices, near_copy(): return lax.ppermute(value, ('macro_2', 'macro_3'), pairs)  7.53 us
    all_to_all x1, waiting for transfers between devices, shards(): lax.all_to_all(rows.reshape(group, 2, 128), GROUP, split_axis=0, concat_a...  7.49 us
    ppermute x4, starting transfers between devices, near_copy(): return lax.ppermute(value, ('macro_2', 'macro_3'), pairs)  5.47 us
  transfers between devices with their start and end apart: 15, of which 10 were waited for; matrix products, arithmetic and copies ran while one was open for 0% of the time, Pallas kernels for 16%

profile of v3, /device:TPU:4, one launch (start us, length us, event | category | flops | bytes accessed | tf_op | source)
XLA Modules:
  0.0 110.4 jit_solution(12137538068982124587)
XLA Ops:
  0.6 1.7 %shard_map.86._ = bf16[384,256]{1,0:T(8,128)(2,1)} custom-call(bf16[12,512,256]{2,1,0:T(8,128)(2,1)} %bitcast.9, bf16[512,256]{1,0:T(8,128)(2,1)} %prop.3, f32[128,256]{1,0:T(8,128)} %fmap.3, f32[128,256]{1,0:T(8,128)} %refs_6_.1), custom_call_target="tpu_custom_call" | custom-call | bytes 3670016 | tf_op jit(solution)/shard_map/pallas_call | solution.py:31
  2.4 2.3 %collective-permute-start.1 = (bf16[384,256]{1,0:T(8,128)(2,1)}, bf16[384,256]{1,0:T(8,128)(2,1)S(1)}, u32[]{:S(2)}, u32[]{:S(2)}) collective-permute-start(bf16[384,256]{1,0:T(8,128)(2,1)} %shard_map.86._), channel_id=1, source_target_pairs={{0,1},{1,0},{2,3},{3,2},{4,5},{5,4},{6,7},{7,6},{8,9},{9,8},{10,11... | collective-permute-start | bytes 589832 | tf_op jit(solution)/shard_map/ppermute | solution.py:314
  4.7 2.4 %shard_map.87 = (bf16[2,256,256]{2,1,0:T(8,128)(2,1)}, bf16[5,256,256]{2,1,0:T(8,128)(2,1)}, bf16[3,256,256]{2,1,0:T(8,128)(2,1)}, bf16[1,256,256]{2,1,0:T(8,128)(2,1)}) custom-call(bf16[12,512,256]{2,1,0:T(8,128)(2,1)} %bitcast.10, bf16[384,256]{1,0:T(8,128)(2,1)} %shard_map.86._), custom_call_target="tpu_custom_call" | custom-call | bytes 3342336 | tf_op jit(solution)/shard_map/pallas_call | solution.py:31
  7.1 1.4 %collective-permute-start.7 = (bf16[5,256,256]{2,1,0:T(8,128)(2,1)}, bf16[5,256,256]{2,1,0:T(8,128)(2,1)S(1)}, u32[]{:S(2)}, u32[]{:S(2)}) collective-permute-start(bf16[5,256,256]{2,1,0:T(8,128)(2,1)} %get-tuple-element.26), channel_id=1, source_target_pairs={{0,1},{1,0},{2,3},{3,2},{4,5},{5,4},{6,7},{7,6},{8,9},{9,8},{10,11... | collective-permute-start | bytes 1966088 | tf_op jit(solution)/shard_map/ppermute | solution.py:314
  8.5 3.4 %collective-permute-done.1.refs_0_ = bf16[384,256]{1,0:T(8,128)(2,1)S(1)} collective-permute-done((bf16[384,256]{1,0:T(8,128)(2,1)}, bf16[384,256]{1,0:T(8,128)(2,1)S(1)}, u32[]{:S(2)}, u32[]{:S(2)}) %collective-permute-start.1) | collective-permute-done | bytes 196640 | tf_op jit(solution)/shard_map/ppermute | solution.py:314
  12.0 3.4 %collective-permute-start.2 = (bf16[128,256]{1,0:T(8,128)(2,1)S(1)}, bf16[128,256]{1,0:T(8,128)(2,1)S(1)}, u32[]{:S(2)}, u32[]{:S(2)}) collective-permute-start(bf16[128,256]{1,0:T(8,128)(2,1)S(1)} %get-tuple-element.43), channel_id=1, source_target_pairs={{0,8},{2,10},{4,12},{6,14},{8,0},{10,2},{12,4},{14,6},{16,24},{18,... | collective-permute-start | bytes 196616 | tf_op jit(solution)/shard_map/ppermute | solution.py:321
  15.3 2.2 %collective-permute-done.2 = bf16[128,256]{1,0:T(8,128)(2,1)S(1)} collective-permute-done((bf16[128,256]{1,0:T(8,128)(2,1)S(1)}, bf16[128,256]{1,0:T(8,128)(2,1)S(1)}, u32[]{:S(2)}, u32[]{:S(2)}) %collective-permute-start.2) | collective-permute-done | bytes 65568 | tf_op jit(solution)/shard_map/ppermute | solution.py:321
  17.7 2.0 %collective-permute-start.4 = (bf16[2,128,256]{2,1,0:T(8,128)(2,1)S(1)}, bf16[2,128,256]{2,1,0:T(8,128)(2,1)S(1)}, u32[]{:S(2)}, u32[]{:S(2)}) collective-permute-start(bf16[2,128,256]{2,1,0:T(8,128)(2,1)S(1)} %pad_maximum_fusion.s0), channel_id=1, source_target_pairs={{0,4},{2,6},{4,0},{6,2},{8,12},{10,14},{12,8},{14,10},{16,20},{18,... | collective-permute-start | bytes 393224 | tf_op jit(solution)/shard_map/ppermute | solution.py:321
  19.7 3.3 %collective-permute-done.5.s3 = bf16[2,128,256]{2,1,0:T(8,128)(2,1)S(1)} collective-permute-done((bf16[2,128,256]{2,1,0:T(8,128)(2,1)S(1)}, bf16[2,128,256]{2,1,0:T(8,128)(2,1)S(1)}, u32[]{:S(2)}, u32[]{:S(2)}) %collective-permute-start.5) | collective-permute-done | bytes 131104 | tf_op jit(solution)/shard_map/ppermute | solution.py:321
  23.0 1.3 %collective-permute-start = (bf16[1,256,256]{2,1,0:T(8,128)(2,1)}, bf16[1,256,256]{2,1,0:T(8,128)(2,1)S(1)}, u32[]{:S(2)}, u32[]{:S(2)}) collective-permute-start(bf16[1,256,256]{2,1,0:T(8,128)(2,1)} %get-tuple-element.22), channel_id=1, source_target_pairs={{0,1},{1,0},{2,3},{3,2},{4,5},{5,4},{6,7},{7,6},{8,9},{9,8},{10,11... | collective-permute-start | bytes 393224 | tf_op jit(solution)/shard_map/ppermute | solution.py:314
  24.3 2.0 %collective-permute-done.4.s2 = bf16[2,128,256]{2,1,0:T(8,128)(2,1)S(1)} collective-permute-done((bf16[2,128,256]{2,1,0:T(8,128)(2,1)S(1)}, bf16[2,128,256]{2,1,0:T(8,128)(2,1)S(1)}, u32[]{:S(2)}, u32[]{:S(2)}) %collective-permute-start.4) | collective-permute-done | bytes 131104 | tf_op jit(solution)/shard_map/ppermute | solution.py:321
  26.3 1.3 %collective-permute-start.6 = (bf16[3,256,256]{2,1,0:T(8,128)(2,1)}, bf16[3,256,256]{2,1,0:T(8,128)(2,1)S(1)}, u32[]{:S(2)}, u32[]{:S(2)}) collective-permute-start(bf16[3,256,256]{2,1,0:T(8,128)(2,1)} %get-tuple-element.25), channel_id=1, source_target_pairs={{0,1},{1,0},{2,3},{3,2},{4,5},{5,4},{6,7},{7,6},{8,9},{9,8},{10,11... | collective-permute-start | bytes 1179656 | tf_op jit(solution)/shard_map/ppermute | solution.py:314
  27.6 0.7 shard_map.88
  28.3 3.9 %collective-permute-done.8.refs_1_ = bf16[2,256,256]{2,1,0:T(8,128)(2,1)S(1)} collective-permute-done((bf16[2,256,256]{2,1,0:T(8,128)(2,1)}, bf16[2,256,256]{2,1,0:T(8,128)(2,1)S(1)}, u32[]{:S(2)}, u32[]{:S(2)}) %collective-permute-start.8) | collective-permute-done | bytes 262176 | tf_op jit(solution)/shard_map/ppermute | solution.py:314
  32.1 3.6 %shard_map.89 = (bf16[12,512,256]{2,1,0:T(8,128)(2,1)}, bf16[3,256,256]{2,1,0:T(8,128)(2,1)}, f32[256,512]{1,0:T(8,128)S(1)}) custom-call(bf16[12,512,256]{2,1,0:T(8,128)(2,1)S(1)} %bitcast.11, bf16[384,256]{1,0:T(8,128)(2,1)S(1)} %collective-permute-done.1.refs_0_, bf16[2,256,256]{2,1,0:T(8,128)(2,1)S(1)} %collective-permute-done.8.refs_1_, ...), custom_call_target="tpu_custom_call" | custom-call | flops 1610612736 | bytes 4653056 | tf_op jit(solution)/shard_map/pallas_call | solution.py:31
  35.7 4.2 %shard_map.90 = (bf16[12,512,256]{2,1,0:T(8,128)(2,1)}, bf16[9,256,256]{2,1,0:T(8,128)(2,1)S(1)}, f32[256,512]{1,0:T(8,128)S(1)}) custom-call(bf16[12,512,256]{2,1,0:T(8,128)(2,1)S(1)} %bitcast.12, bf16[5,256,256]{2,1,0:T(8,128)(2,1)S(1)} %collective-permute-done.7.refs_0_, ...), custom_call_target="tpu_custom_call", output_to_operand_aliasing={{0}: (4, {}), {2}: (5, {})} | custom-call | flops 2684354560 | bytes 8519680 | tf_op jit(solution)/shard_map/pallas_call | solution.py:31
  39.9 1.8 %collective-permute-done.6.refs_0_ = bf16[3,256,256]{2,1,0:T(8,128)(2,1)S(1)} collective-permute-done((bf16[3,256,256]{2,1,0:T(8,128)(2,1)}, bf16[3,256,256]{2,1,0:T(8,128)(2,1)S(1)}, u32[]{:S(2)}, u32[]{:S(2)}) %collective-permute-start.6) | collective-permute-done | bytes 393248 | tf_op jit(solution)/shard_map/ppermute | solution.py:314
  41.7 3.0 %shard_map.91 = (bf16[12,512,256]{2,1,0:T(8,128)(2,1)}, bf16[9,256,256]{2,1,0:T(8,128)(2,1)S(1)}, f32[256,512]{1,0:T(8,128)S(1)}) custom-call(bf16[12,512,256]{2,1,0:T(8,128)(2,1)S(1)} %bitcast.13, bf16[3,256,256]{2,1,0:T(8,128)(2,1)S(1)} %collective-permute-done.6.refs_0_, ...), custom_call_target="tpu_custom_call", output_to_operand_aliasing={{0}: (4, {}), {2}: (5, {}), {1}: (6, {})} | custom-call | flops 1610612736 | bytes 9437184 | tf_op jit(solution)/shard_map/pallas_call | solution.py:31
  44.8 2.5 %shard_map.92 = (bf16[12,512,256]{2,1,0:T(8,128)(2,1)}, bf16[9,256,256]{2,1,0:T(8,128)(2,1)S(1)}, bf16[272,128]{1,0:T(8,128)(2,1)S(1)}, f32[8,128]{1,0:T(8,128)S(1)}) custom-call(bf16[12,512,256]{2,1,0:T(8,128)(2,1)S(1)} %bitcast.14, bf16[1,256,256]{2,1,0:T(8,128)(2,1)S(1)} %collective-permute-done.refs_0_, ...), custom_call_target="tpu_custom_call", output_to_operand_aliasing={{0}: (4, {}), {1}: (6, {})} | custom-call | flops 536870912 | bytes 9701888 | tf_op jit(solution)/shard_map/pallas_call | solution.py:31
  47.3 1.6 %collective-permute-start.12 = (bf16[9,256,256]{2,1,0:T(8,128)(2,1)S(1)}, bf16[9,256,256]{2,1,0:T(8,128)(2,1)S(1)}, u32[]{:S(2)}, u32[]{:S(2)}) collective-permute-start(bf16[9,256,256]{2,1,0:T(8,128)(2,1)S(1)} %get-tuple-element.39), channel_id=1, source_target_pairs={{0,1},{1,0},{2,3},{3,2},{4,5},{5,4},{6,7},{7,6},{8,9},{9,8},{10,11... | collective-permute-start | bytes 3538952 | tf_op jit(solution)/shard_map/ppermute | solution.py:314
  48.9 2.0 %collective-permute-start.13 = (bf16[3,256,256]{2,1,0:T(8,128)(2,1)}, bf16[3,256,256]{2,1,0:T(8,128)(2,1)}, u32[]{:S(2)}, u32[]{:S(2)}) collective-permute-start(bf16[3,256,256]{2,1,0:T(8,128)(2,1)} %get-tuple-element.40), channel_id=1, source_target_pairs={{0,1},{1,0},{2,3},{3,2},{4,5},{5,4},{6,7},{7,6},{8,9},{9,8},{10,11... | collective-permute-start | bytes 1179656 | tf_op jit(solution)/shard_map/ppermute | solution.py:314
  50.9 1.5 %collective-permute-start.9 = (bf16[272,128]{1,0:T(8,128)(2,1)S(1)}, bf16[272,128]{1,0:T(8,128)(2,1)S(1)}, u32[]{:S(2)}, u32[]{:S(2)}) collective-permute-start(bf16[272,128]{1,0:T(8,128)(2,1)S(1)} %get-tuple-element.38.own), channel_id=1, source_target_pairs={{0,1},{1,0},{2,3},{3,2},{4,5},{5,4},{6,7},{7,6},{8,9},{9,8},{10,11... | collective-permute-start | bytes 208904 | tf_op jit(solution)/shard_map/ppermute | solution.py:314
  52.4 1.1 %collective-permute-start.11 = (f32[8,128]{1,0:T(8,128)S(1)}, f32[8,128]{1,0:T(8,128)S(1)}, u32[]{:S(2)}, u32[]{:S(2)}) collective-permute-start(f32[8,128]{1,0:T(8,128)S(1)} %get-tuple-element.37.own), channel_id=1, source_target_pairs={{0,33},{1,32},{32,1},{33,0},{2,35},{3,34},{34,3},{35,2},{4,37},{5,... | collective-permute-start | bytes 12296 | tf_op jit(solution)/shard_map/ppermute | solution.py:434
  53.5 2.0 %collective-permute-start.10 = (f32[8,128]{1,0:T(8,128)S(1)}, f32[8,128]{1,0:T(8,128)S(1)}, u32[]{:S(2)}, u32[]{:S(2)}) collective-permute-start(f32[8,128]{1,0:T(8,128)S(1)} %get-tuple-element.37.own), channel_id=1, source_target_pairs={{0,32},{32,0},{1,33},{33,1},{2,34},{34,2},{3,35},{35,3},{4,36},{36... | collective-permute-start | bytes 12296 | tf_op jit(solution)/shard_map/ppermute | solution.py:433
  55.6 0.8 collective-permute-done.11.both
  56.4 28.3 %collective-permute-done.10.beside = f32[8,128]{1,0:T(8,128)S(1)} collective-permute-done((f32[8,128]{1,0:T(8,128)S(1)}, f32[8,128]{1,0:T(8,128)S(1)}, u32[]{:S(2)}, u32[]{:S(2)}) %collective-permute-start.10) | collective-permute-done | bytes 4128 | tf_op jit(solution)/shard_map/ppermute | solution.py:433
  85.2 0.7 shard_map.93
  85.9 12.6 %all-to-all-start = ((f32[64,2,128]{2,1,0:T(2,128)}), f32[64,2,128]{2,1,0:T(2,128)S(1)}, u32[]{:S(2)}, u32[]{:S(2)}) async-start(f32[64,2,128]{2,1,0:T(2,128)} %bitcast.5), calls=%async_computation | async-start | bytes 131072 | tf_op jit(solution)/shard_map/all_to_all | solution.py:443
  99.0 1.8 %shard_map.96._ = bf16[12,512,256]{2,1,0:T(8,128)(2,1)} custom-call(bf16[3,256,256]{2,1,0:T(8,128)(2,1)} %collective-permute-done.13.array, bf16[12,512,256]{2,1,0:T(8,128)(2,1)} %get-tuple-element.41._), custom_call_target="tpu_custom_call", output_to_operand_aliasing={{}: (1, {})} | custom-call | bytes 3538944 | tf_op jit(solution)/shard_map/pallas_call | solution.py:31
  100.7 7.5 %all-to-all-done = f32[64,2,128]{2,1,0:T(2,128)S(1)} async-done(((f32[64,2,128]{2,1,0:T(2,128)}), f32[64,2,128]{2,1,0:T(2,128)S(1)}, u32[]{:S(2)}, u32[]{:S(2)}) %all-to-all-start) | async-done | bytes 65568 | tf_op jit(solution)/shard_map/all_to_all | solution.py:443
  108.2 0.9 shard_map.95
  109.2 1.1 shard_map.97
  (26 shorter events, 1.1 us)
Async XLA Ops:
  0.6 26.9 %copy-start.4 = (f32[128,256]{1,0:T(8,128)S(1)}, f32[128,256]{1,0:T(8,128)}, u32[]{:S(2)}) copy-start(f32[128,256]{1,0:T(8,128)} %fmap.3) | copy-start | bytes 393220
  2.3 25.2 %copy-start.1 = (f32[512,128]{1,0:T(8,128)S(1)}, f32[512,128]{1,0:T(8,128)}, u32[]{:S(2)}) copy-start(f32[512,128]{1,0:T(8,128)} %macro.3) | copy-start | bytes 786436
  2.4 25.2 %copy-start.2 = (bf16[512,256]{1,0:T(8,128)(2,1)S(1)}, bf16[512,256]{1,0:T(8,128)(2,1)}, u32[]{:S(2)}) copy-start(bf16[512,256]{1,0:T(8,128)(2,1)} %prop.3) | copy-start | bytes 786436
  2.4 29.8 %copy-start = (bf16[512,12,256]{2,0,1:T(8,128)(2,1)S(1)}, bf16[512,12,256]{2,0,1:T(8,128)(2,1)}, u32[]{:S(2)}) copy-start(bf16[512,12,256]{2,0,1:T(8,128)(2,1)} %param.8) | copy-start | bytes 9437188
  2.4 9.6 %collective-permute-start.1 = (bf16[384,256]{1,0:T(8,128)(2,1)}, bf16[384,256]{1,0:T(8,128)(2,1)S(1)}, u32[]{:S(2)}, u32[]{:S(2)}) collective-permute-start(bf16[384,256]{1,0:T(8,128)(2,1)} %shard_map.86._), channel_id=1, source_target_pairs={{0,1},{1,0},{2,3},{3,2},{4,5},{5,4},{6,7},{7,6},{8,9},{9,8},{10,11... | collective-permute-start | bytes 589832 | tf_op jit(solution)/shard_map/ppermute | solution.py:314
  7.1 28.6 %collective-permute-start.7 = (bf16[5,256,256]{2,1,0:T(8,128)(2,1)}, bf16[5,256,256]{2,1,0:T(8,128)(2,1)S(1)}, u32[]{:S(2)}, u32[]{:S(2)}) collective-permute-start(bf16[5,256,256]{2,1,0:T(8,128)(2,1)} %get-tuple-element.26), channel_id=1, source_target_pairs={{0,1},{1,0},{2,3},{3,2},{4,5},{5,4},{6,7},{7,6},{8,9},{9,8},{10,11... | collective-permute-start | bytes 1966088 | tf_op jit(solution)/shard_map/ppermute | solution.py:314
  12.0 5.6 %collective-permute-start.2 = (bf16[128,256]{1,0:T(8,128)(2,1)S(1)}, bf16[128,256]{1,0:T(8,128)(2,1)S(1)}, u32[]{:S(2)}, u32[]{:S(2)}) collective-permute-start(bf16[128,256]{1,0:T(8,128)(2,1)S(1)} %get-tuple-element.43), channel_id=1, source_target_pairs={{0,8},{2,10},{4,12},{6,14},{8,0},{10,2},{12,4},{14,6},{16,24},{18,... | collective-permute-start | bytes 196616 | tf_op jit(solution)/shard_map/ppermute | solution.py:321
  15.3 16.8 %collective-permute-start.8 = (bf16[2,256,256]{2,1,0:T(8,128)(2,1)}, bf16[2,256,256]{2,1,0:T(8,128)(2,1)S(1)}, u32[]{:S(2)}, u32[]{:S(2)}) collective-permute-start(bf16[2,256,256]{2,1,0:T(8,128)(2,1)} %get-tuple-element.27), channel_id=1, source_target_pairs={{0,1},{1,0},{2,3},{3,2},{4,5},{5,4},{6,7},{7,6},{8,9},{9,8},{10,11... | collective-permute-start | bytes 786440 | tf_op jit(solution)/shard_map/ppermute | solution.py:314
  17.6 5.4 %collective-permute-start.5 = (bf16[2,128,256]{2,1,0:T(8,128)(2,1)S(1)}, bf16[2,128,256]{2,1,0:T(8,128)(2,1)S(1)}, u32[]{:S(2)}, u32[]{:S(2)}) collective-permute-start(bf16[2,128,256]{2,1,0:T(8,128)(2,1)S(1)} %pad_maximum_fusion.s0), channel_id=1, source_target_pairs={{0,6},{2,4},{4,2},{6,0},{8,14},{10,12},{12,10},{14,8},{16,22},{18,... | collective-permute-start | bytes 393224 | tf_op jit(solution)/shard_map/ppermute | solution.py:321
  17.7 8.6 %collective-permute-start.4 = (bf16[2,128,256]{2,1,0:T(8,128)(2,1)S(1)}, bf16[2,128,256]{2,1,0:T(8,128)(2,1)S(1)}, u32[]{:S(2)}, u32[]{:S(2)}) collective-permute-start(bf16[2,128,256]{2,1,0:T(8,128)(2,1)S(1)} %pad_maximum_fusion.s0), channel_id=1, source_target_pairs={{0,4},{2,6},{4,0},{6,2},{8,12},{10,14},{12,8},{14,10},{16,20},{18,... | collective-permute-start | bytes 393224 | tf_op jit(solution)/shard_map/ppermute | solution.py:321
  19.7 7.9 %collective-permute-start.3 = (bf16[2,128,256]{2,1,0:T(8,128)(2,1)S(1)}, bf16[2,128,256]{2,1,0:T(8,128)(2,1)S(1)}, u32[]{:S(2)}, u32[]{:S(2)}) collective-permute-start(bf16[2,128,256]{2,1,0:T(8,128)(2,1)S(1)} %pad_maximum_fusion.s0), channel_id=1, source_target_pairs={{0,2},{2,0},{4,6},{6,4},{8,10},{10,8},{12,14},{14,12},{16,18},{18,... | collective-permute-start | bytes 393224 | tf_op jit(solution)/shard_map/ppermute | solution.py:321
  23.0 21.7 %collective-permute-start = (bf16[1,256,256]{2,1,0:T(8,128)(2,1)}, bf16[1,256,256]{2,1,0:T(8,128)(2,1)S(1)}, u32[]{:S(2)}, u32[]{:S(2)}) collective-permute-start(bf16[1,256,256]{2,1,0:T(8,128)(2,1)} %get-tuple-element.22), channel_id=1, source_target_pairs={{0,1},{1,0},{2,3},{3,2},{4,5},{5,4},{6,7},{7,6},{8,9},{9,8},{10,11... | collective-permute-start | bytes 393224 | tf_op jit(solution)/shard_map/ppermute | solution.py:314
  26.3 15.4 %collective-permute-start.6 = (bf16[3,256,256]{2,1,0:T(8,128)(2,1)}, bf16[3,256,256]{2,1,0:T(8,128)(2,1)S(1)}, u32[]{:S(2)}, u32[]{:S(2)}) collective-permute-start(bf16[3,256,256]{2,1,0:T(8,128)(2,1)} %get-tuple-element.25), channel_id=1, source_target_pairs={{0,1},{1,0},{2,3},{3,2},{4,5},{5,4},{6,7},{7,6},{8,9},{9,8},{10,11... | collective-permute-start | bytes 1179656 | tf_op jit(solution)/shard_map/ppermute | solution.py:314
  41.7 3.0 %copy-start.3 = (f32[128,256]{1,0:T(8,128)S(1)}, f32[128,256]{1,0:T(8,128)}, u32[]{:S(2)}) copy-start(f32[128,256]{1,0:T(8,128)} %refs_6_.1) | copy-start | bytes 393220
  41.7 3.0 %copy-start.5 = (f32[512]{0:T(512)S(1)}, f32[512]{0:T(512)}, u32[]{:S(2)}) copy-start(f32[512]{0:T(512)} %param.9) | copy-start | bytes 6148
  41.7 3.0 %copy-start.6 = (f32[128]{0:T(128)S(1)}, f32[128]{0:T(128)}, u32[]{:S(2)}) copy-start(f32[128]{0:T(128)} %param.13) | copy-start | bytes 1540
  47.3 61.9 %collective-permute-start.12 = (bf16[9,256,256]{2,1,0:T(8,128)(2,1)S(1)}, bf16[9,256,256]{2,1,0:T(8,128)(2,1)S(1)}, u32[]{:S(2)}, u32[]{:S(2)}) collective-permute-start(bf16[9,256,256]{2,1,0:T(8,128)(2,1)S(1)} %get-tuple-element.39), channel_id=1, source_target_pairs={{0,1},{1,0},{2,3},{3,2},{4,5},{5,4},{6,7},{7,6},{8,9},{9,8},{10,11... | collective-permute-start | bytes 3538952 | tf_op jit(solution)/shard_map/ppermute | solution.py:314
  48.9 50.1 %collective-permute-start.13 = (bf16[3,256,256]{2,1,0:T(8,128)(2,1)}, bf16[3,256,256]{2,1,0:T(8,128)(2,1)}, u32[]{:S(2)}, u32[]{:S(2)}) collective-permute-start(bf16[3,256,256]{2,1,0:T(8,128)(2,1)} %get-tuple-element.40), channel_id=1, source_target_pairs={{0,1},{1,0},{2,3},{3,2},{4,5},{5,4},{6,7},{7,6},{8,9},{9,8},{10,11... | collective-permute-start | bytes 1179656 | tf_op jit(solution)/shard_map/ppermute | solution.py:314
  50.9 34.3 %collective-permute-start.9 = (bf16[272,128]{1,0:T(8,128)(2,1)S(1)}, bf16[272,128]{1,0:T(8,128)(2,1)S(1)}, u32[]{:S(2)}, u32[]{:S(2)}) collective-permute-start(bf16[272,128]{1,0:T(8,128)(2,1)S(1)} %get-tuple-element.38.own), channel_id=1, source_target_pairs={{0,1},{1,0},{2,3},{3,2},{4,5},{5,4},{6,7},{7,6},{8,9},{9,8},{10,11... | collective-permute-start | bytes 208904 | tf_op jit(solution)/shard_map/ppermute | solution.py:314
  52.4 3.9 %collective-permute-start.11 = (f32[8,128]{1,0:T(8,128)S(1)}, f32[8,128]{1,0:T(8,128)S(1)}, u32[]{:S(2)}, u32[]{:S(2)}) collective-permute-start(f32[8,128]{1,0:T(8,128)S(1)} %get-tuple-element.37.own), channel_id=1, source_target_pairs={{0,33},{1,32},{32,1},{33,0},{2,35},{3,34},{34,3},{35,2},{4,37},{5,... | collective-permute-start | bytes 12296 | tf_op jit(solution)/shard_map/ppermute | solution.py:434
  53.5 31.1 %collective-permute-start.10 = (f32[8,128]{1,0:T(8,128)S(1)}, f32[8,128]{1,0:T(8,128)S(1)}, u32[]{:S(2)}, u32[]{:S(2)}) collective-permute-start(f32[8,128]{1,0:T(8,128)S(1)} %get-tuple-element.37.own), channel_id=1, source_target_pairs={{0,32},{32,0},{1,33},{33,1},{2,34},{34,2},{3,35},{35,3},{4,36},{36... | collective-permute-start | bytes 12296 | tf_op jit(solution)/shard_map/ppermute | solution.py:433
  85.9 22.3 %all-to-all-start = ((f32[64,2,128]{2,1,0:T(2,128)}), f32[64,2,128]{2,1,0:T(2,128)S(1)}, u32[]{:S(2)}, u32[]{:S(2)}) async-start(f32[64,2,128]{2,1,0:T(2,128)} %bitcast.5), calls=%async_computation | async-start | bytes 131072 | tf_op jit(solution)/shard_map/all_to_all | solution.py:443
